TPU v7x, 32 devices: a whole 2x2x4 slice. The times are simulated.
32 devices in a mesh: item: 4 (over z), var: 8 (over y, x, core).
Axes of the slice: x: 2, y: 2, z: 4, core: 2. Of those that a mesh axis runs over, the one named last changes fastest.
Arguments:
- pixels: bfloat16 [4, 64, 4, 2048], P('item', 'var'), may hold values from -6 to 6
- dataset: int32 [4], P('item'), may hold values from 0 to 4
- var_mask: int32 [5, 64], replicated, may hold values from 0 to 1, as said below
- data_weight: int32 [5], replicated, may hold values from 1 to 9
- emb_weight: bfloat16 [64, 4, 1024], P('var'), may hold values from -3 to 3
- var_embed: bfloat16 [64, 1024], P('var'), may hold values from -6 to 6
- agg_query: bfloat16 [1024], replicated, may hold values from -6 to 6
- agg_key: bfloat16 [1024, 1024], replicated, may hold values from -0.1875 to 0.1875
- agg_value: bfloat16 [1024, 1024], replicated, may hold values from -0.1875 to 0.1875
- agg_out: bfloat16 [1024, 1024], replicated, may hold values from -0.1875 to 0.1875
- ln1_gain: bfloat16 [1024], replicated, may hold values from 0.5 to 1.5
- ln1_bias: bfloat16 [1024], replicated, may hold values from -3 to 3
- qkv_weight: bfloat16 [1024, 3072], replicated, may hold values from -0.25 to 0.25
- proj_weight: bfloat16 [1024, 1024], replicated, may hold values from -0.75 to 0.75
- ln2_gain: bfloat16 [1024], replicated, may hold values from 0.5 to 1.5
- ln2_bias: bfloat16 [1024], replicated, may hold values from -3 to 3
- fc1_weight: bfloat16 [1024, 4096], replicated, may hold values from -0.1875 to 0.1875
- fc1_bias: bfloat16 [4096], replicated, may hold values from -3 to 3
- fc2_weight: bfloat16 [4096, 1024], replicated, may hold values from -0.09375 to 0.09375
- fc2_bias: bfloat16 [1024], replicated, may hold values from -3 to 3
- cotangent: bfloat16 [4, 2048, 1024], P('item', 'var'), may hold values from -6 to 6
Outputs:
- block_output: bfloat16 [4, 2048, 1024], P('item', 'var')
- pixels_grad: bfloat16 [4, 64, 4, 2048], P('item', 'var')
- emb_weight_grad: float32 [64, 4, 1024], P('var')
- var_embed_grad: float32 [64, 1024], P('var')
- agg_query_grad: float32 [1024], P('var')
- agg_key_grad: float32 [1024, 1024], P(None, 'var')
- agg_value_grad: float32 [1024, 1024], P(None, 'var')
- agg_out_grad: float32 [1024, 1024], P(None, 'var')
- ln1_gain_grad: float32 [1024], P('var')
- ln1_bias_grad: float32 [1024], P('var')
- qkv_weight_grad: float32 [1024, 3072], P(None, 'var')
- proj_weight_grad: float32 [1024, 1024], P(None, 'var')
- ln2_gain_grad: float32 [1024], P('var')
- ln2_bias_grad: float32 [1024], P('var')
- fc1_weight_grad: float32 [1024, 4096], P(None, 'var')
- fc1_bias_grad: float32 [4096], P('var')
- fc2_weight_grad: float32 [4096, 1024], P(None, 'var')
- fc2_bias_grad: float32 [1024], P('var')
Inputs may be any that keep to these rules, and one draw needn't show every extreme that they name: `var_mask`: each dataset's list names at least one variable; no list names a slot whose index is 3 mod 4.
All inputs are finite; a program needn't handle non-finite values.
Results may differ from a plain program's by a relative error of at most 0.025.
Values may be sent and summed in bfloat16 or wider, within the bound.
A program may use at most 512 MiB of HBM per device.

v0:
```python
import jax
import jax.numpy as jnp
from jax import lax
from jax.sharding import PartitionSpec as P

D = 1024
HEADS = 16
HEAD_DIM = 64
PATCHES = 2048
NDATA = 5
KEY_STEPS = 4


PRECISE = lax.Precision.HIGHEST


def layer_norm(values, gain_vec, shift_vec):
    center = values - jnp.mean(values, axis=-1, keepdims=True)
    spread = jnp.mean(center * center, axis=-1, keepdims=True)
    return center * lax.rsqrt(spread + 1e-06) * gain_vec + shift_vec


def exact_gelu(values):
    return jax.nn.gelu(values, approximate=False)


def head_split(values):
    return values.reshape(values.shape[:-1] + (HEADS, HEAD_DIM))


def embed_tokens(pixel_block, table, offsets):
    spread = jnp.einsum("gvcp,vcd->gvpd", pixel_block, table, preferred_element_type=jnp.float32)
    return (spread + offsets.astype(jnp.float32)[None, :, None, :]).astype(jnp.bfloat16)


def aggregate_forward(tokens, head_probe, live_mask):
    factor = HEAD_DIM ** (-0.5)
    agg_scores = (
        jnp.einsum("gvsd,hd->gvsh", tokens, head_probe, preferred_element_type=jnp.float32) * factor
    )
    present = live_mask[:, :, None, None] > 0.5
    masked = jnp.where(present, agg_scores, -1e30)
    highest = jnp.max(masked, axis=1, keepdims=True)
    exp_terms = jnp.exp(masked - highest) * live_mask[:, :, None, None]
    agg_weights = exp_terms / jnp.sum(exp_terms, axis=1, keepdims=True)
    weights_low = agg_weights.astype(jnp.bfloat16)
    context = jnp.einsum("gvsh,gvsd->gshd", weights_low, tokens, preferred_element_type=jnp.float32)
    return (agg_weights, weights_low, context.astype(jnp.bfloat16))


def aggregate_back(item_args, head_probe):
    tokens, agg_weights, weights_low, g_context = item_args
    factor = HEAD_DIM ** (-0.5)
    g_weights = jnp.einsum("shd,vsd->vsh", g_context, tokens, preferred_element_type=jnp.float32)
    rowdot = jnp.sum(agg_weights * g_weights, axis=0, keepdims=True)
    g_scores = (agg_weights * (g_weights - rowdot)).astype(jnp.bfloat16)
    g_tokens = jnp.einsum(
        "vsh,shd->vsd", weights_low, g_context, preferred_element_type=jnp.float32
    )
    g_tokens = (
        g_tokens
        + jnp.einsum("vsh,hd->vsd", g_scores, head_probe, preferred_element_type=jnp.float32)
        * factor
    )
    g_probe = (
        jnp.einsum("vsh,vsd->hd", g_scores, tokens, preferred_element_type=jnp.float32) * factor
    )
    return (g_tokens.astype(jnp.bfloat16), g_probe)


def key_block_grads(queries, g_attended, log_total, rowdot, key_piece):
    factor = HEAD_DIM ** (-0.5)
    block_keys = key_piece[:, :, 0]
    block_values = key_piece[:, :, 1]
    scores = (
        jnp.einsum("gshe,gkhe->ghsk", queries, block_keys, preferred_element_type=jnp.float32)
        * factor
    )
    block_probs = jnp.exp(scores - log_total)
    g_probs = jnp.einsum(
        "gshe,gkhe->ghsk", g_attended, block_values, preferred_element_type=jnp.float32
    )
    g_scores = (block_probs * (g_probs - rowdot)).astype(jnp.bfloat16)
    g_queries = (
        jnp.einsum("ghsk,gkhe->gshe", g_scores, block_keys, preferred_element_type=jnp.float32)
        * factor
    )
    g_keys = (
        jnp.einsum("ghsk,gshe->gkhe", g_scores, queries, preferred_element_type=jnp.float32)
        * factor
    )
    g_values = jnp.einsum(
        "ghsk,gshe->gkhe",
        block_probs.astype(jnp.bfloat16),
        g_attended,
        preferred_element_type=jnp.float32,
    )
    return (g_queries, jnp.stack([g_keys, g_values], axis=2))


def body(
    pixels,
    dataset,
    var_mask,
    data_weight,
    emb_weight,
    var_embed,
    agg_query,
    agg_key,
    agg_value,
    agg_out,
    ln1_gain,
    ln1_bias,
    qkv_weight,
    proj_weight,
    ln2_gain,
    ln2_bias,
    fc1_weight,
    fc1_bias,
    fc2_weight,
    fc2_bias,
    cotangent,
):
    groups = pixels.shape[0]
    lane_count = lax.axis_size("var")
    patch_share = PATCHES // lane_count
    row_count = groups * patch_share
    block_width = patch_share // KEY_STEPS
    factor = HEAD_DIM ** (-0.5)
    dataset_hot = (dataset[:, None] == jnp.arange(NDATA, dtype=jnp.int32)[None, :]).astype(
        jnp.float32
    )
    counts = data_weight.astype(jnp.float32)
    item_scale = jnp.dot(dataset_hot, counts, precision=PRECISE) * NDATA / jnp.sum(counts)
    live_mask = jnp.dot(dataset_hot, var_mask.astype(jnp.float32), precision=PRECISE)
    local_tokens = embed_tokens(pixels, emb_weight, var_embed)
    tokens = lax.all_to_all(local_tokens, "var", split_axis=2, concat_axis=1, tiled=True)
    query_full = agg_query.astype(jnp.float32)
    key_full = agg_key.astype(jnp.float32)
    head_probe = (
        (key_full * query_full[None, :])
        .reshape(D, HEADS, HEAD_DIM)
        .sum(axis=-1)
        .T.astype(jnp.bfloat16)
    )
    agg_weights, weights_low, context = aggregate_forward(tokens, head_probe, live_mask)
    value_heads = agg_value.reshape(D, HEADS, HEAD_DIM)
    agg_mixed = jnp.einsum(
        "gshd,dhe->gshe", context, value_heads, preferred_element_type=jnp.float32
    )
    agg_mixed = agg_mixed.astype(jnp.bfloat16).reshape(row_count, D)
    agg_result = jnp.dot(agg_mixed, agg_out, preferred_element_type=jnp.float32)
    small_params = tuple(
        (
            vector.astype(jnp.float32)
            for vector in (ln1_gain, ln1_bias, ln2_gain, ln2_bias, fc1_bias, fc2_bias)
        )
    )
    first_norm = layer_norm(agg_result, small_params[0], small_params[1]).astype(jnp.bfloat16)
    qkv_proj = jnp.dot(first_norm, qkv_weight, preferred_element_type=jnp.float32).astype(
        jnp.bfloat16
    )
    qkv_proj = qkv_proj.reshape(groups, patch_share, 3 * D)
    queries = head_split(qkv_proj[..., :D])
    keyval = qkv_proj[..., D:]
    gathered = lax.all_gather(keyval, "var", axis=1, tiled=True)
    all_keys = head_split(gathered[..., :D])
    all_values = head_split(gathered[..., D:])
    scores = (
        jnp.einsum("gshe,gkhe->ghsk", queries, all_keys, preferred_element_type=jnp.float32)
        * factor
    )
    highest = jnp.max(scores, axis=-1, keepdims=True)
    exp_terms = jnp.exp(scores - highest)
    totals = jnp.sum(exp_terms, axis=-1, keepdims=True)
    probs_low = (exp_terms / totals).astype(jnp.bfloat16)
    log_total = highest + jnp.log(totals)
    attended_full = jnp.einsum(
        "ghsk,gkhe->gshe", probs_low, all_values, preferred_element_type=jnp.float32
    )
    attended = attended_full.astype(jnp.bfloat16).reshape(row_count, D)
    residual = agg_result + jnp.dot(attended, proj_weight, preferred_element_type=jnp.float32)
    second_norm = layer_norm(residual, small_params[2], small_params[3]).astype(jnp.bfloat16)
    pre_act = jnp.dot(second_norm, fc1_weight, preferred_element_type=jnp.float32) + small_params[4]
    gelu_out, gelu_pull = jax.vjp(exact_gelu, pre_act)
    gelu_low = gelu_out.astype(jnp.bfloat16)
    block_out = (
        residual
        + jnp.dot(gelu_low, fc2_weight, preferred_element_type=jnp.float32)
        + small_params[5]
    )
    g_final = (cotangent.astype(jnp.float32) * item_scale[:, None, None]).reshape(row_count, D)
    g_mlp = g_final.astype(jnp.bfloat16)
    fc2_grad = jnp.einsum("rf,rd->fd", gelu_low, g_mlp, preferred_element_type=jnp.float32)
    fc2_bias_grad = jnp.sum(g_mlp, axis=0, dtype=jnp.float32)
    g_gelu = jnp.einsum("rd,fd->rf", g_mlp, fc2_weight, preferred_element_type=jnp.float32)
    g_pre = gelu_pull(g_gelu)[0].astype(jnp.bfloat16)
    fc1_grad = jnp.einsum("rd,rf->df", second_norm, g_pre, preferred_element_type=jnp.float32)
    fc1_bias_grad = jnp.sum(g_pre, axis=0, dtype=jnp.float32)
    g_second = jnp.einsum("rf,df->rd", g_pre, fc1_weight, preferred_element_type=jnp.float32)
    second_pull = jax.vjp(layer_norm, residual, small_params[2], small_params[3])[1]
    g_resid_norm, ln2_gain_grad, ln2_bias_grad = second_pull(g_second)
    g_residual = g_final + g_resid_norm
    g_branch = g_residual.astype(jnp.bfloat16)
    proj_grad = jnp.einsum("rd,re->de", attended, g_branch, preferred_element_type=jnp.float32)
    g_attended = jnp.einsum("re,de->rd", g_branch, proj_weight, preferred_element_type=jnp.float32)
    g_attended = head_split(g_attended.astype(jnp.bfloat16).reshape(groups, patch_share, D))
    rowdot = jnp.sum(g_attended.astype(jnp.float32) * attended_full, axis=-1)
    rowdot = jnp.transpose(rowdot, (0, 2, 1))[..., None]
    key_blocks = gathered.reshape(groups, lane_count, patch_share, 2 * D)
    g_query_sum = jnp.zeros((groups, patch_share, HEADS, HEAD_DIM), jnp.float32)
    for block_index in range(KEY_STEPS):
        key_piece = key_blocks[:, :, block_index * block_width : (block_index + 1) * block_width]
        key_piece = key_piece.reshape(groups, lane_count * block_width, 2, HEADS, HEAD_DIM)
        g_queries, grad_term = key_block_grads(queries, g_attended, log_total, rowdot, key_piece)
        g_query_sum = g_query_sum + g_queries
    total_rows = jnp.transpose(log_total[..., 0], (0, 2, 1))
    rowdot_rows = jnp.transpose(rowdot[..., 0], (0, 2, 1))
    side_queries, side_grads = (
        lax.all_gather(queries.reshape(groups, patch_share, D), "var", axis=1, tiled=True),
        lax.all_gather(g_attended.reshape(groups, patch_share, D), "var", axis=1, tiled=True),
    )
    side_total, side_rowdot = (
        lax.all_gather(total_rows, "var", axis=1, tiled=True),
        lax.all_gather(rowdot_rows, "var", axis=1, tiled=True),
    )
    query_blocks = side_queries.reshape(groups, lane_count, patch_share, D)
    grad_blocks = side_grads.reshape(groups, lane_count, patch_share, D)
    total_blocks = side_total.reshape(groups, lane_count, patch_share, HEADS)
    rowdot_blocks = side_rowdot.reshape(groups, lane_count, patch_share, HEADS)
    own_piece = keyval.reshape(groups, patch_share, 2, HEADS, HEAD_DIM)
    g_keyval_sum = jnp.zeros((groups, patch_share, 2, HEADS, HEAD_DIM), jnp.float32)
    for block_index in range(KEY_STEPS):
        lower = block_index * block_width
        upper = lower + block_width
        block_queries = head_split(
            query_blocks[:, :, lower:upper].reshape(groups, lane_count * block_width, D)
        )
        block_grads = head_split(
            grad_blocks[:, :, lower:upper].reshape(groups, lane_count * block_width, D)
        )
        block_total = total_blocks[:, :, lower:upper].reshape(
            groups, lane_count * block_width, HEADS
        )
        block_rowdot = rowdot_blocks[:, :, lower:upper].reshape(
            groups, lane_count * block_width, HEADS
        )
        block_total = jnp.transpose(block_total, (0, 2, 1))[..., None]
        block_rowdot = jnp.transpose(block_rowdot, (0, 2, 1))[..., None]
        unused_grads, grad_term = key_block_grads(
            block_queries, block_grads, block_total, block_rowdot, own_piece
        )
        g_keyval_sum = g_keyval_sum + grad_term
    g_keyval = g_keyval_sum.reshape(groups, patch_share, 2 * D)
    g_qkv = jnp.concatenate([g_query_sum.reshape(groups, patch_share, D), g_keyval], axis=-1)
    g_qkv = g_qkv.astype(jnp.bfloat16).reshape(row_count, 3 * D)
    qkv_grad = jnp.einsum("rd,re->de", first_norm, g_qkv, preferred_element_type=jnp.float32)
    g_first = jnp.einsum("re,de->rd", g_qkv, qkv_weight, preferred_element_type=jnp.float32)
    first_pull = jax.vjp(layer_norm, agg_result, small_params[0], small_params[1])[1]
    g_result_norm, ln1_gain_grad, ln1_bias_grad = first_pull(g_first)
    g_result = (g_residual + g_result_norm).astype(jnp.bfloat16)
    agg_out_grad = jnp.einsum("rj,rd->jd", agg_mixed, g_result, preferred_element_type=jnp.float32)
    g_mixed = jnp.einsum("rd,jd->rj", g_result, agg_out, preferred_element_type=jnp.float32)
    g_mixed = head_split(g_mixed.astype(jnp.bfloat16).reshape(groups, patch_share, D))
    agg_value_grad = jnp.einsum(
        "gshd,gshe->dhe", context, g_mixed, preferred_element_type=jnp.float32
    ).reshape(D, D)
    g_context = jnp.einsum(
        "gshe,dhe->gshd", g_mixed, value_heads, preferred_element_type=jnp.float32
    )
    g_context = g_context.astype(jnp.bfloat16)

    def back_item(item_args):
        return aggregate_back(item_args, head_probe)

    g_tokens, probe_parts = lax.map(back_item, (tokens, agg_weights, weights_low, g_context))
    g_probe = jnp.sum(probe_parts, axis=0)
    g_probe_cols = jnp.repeat(g_probe.T, HEAD_DIM, axis=1)
    agg_key_grad = g_probe_cols * query_full[None, :]
    agg_query_grad = jnp.sum(g_probe_cols * key_full, axis=0)
    home_grads = lax.all_to_all(g_tokens, "var", split_axis=1, concat_axis=2, tiled=True)
    table_part = jnp.einsum(
        "gvcp,gvpd->vcd", pixels, home_grads, preferred_element_type=jnp.float32
    )
    offset_part = jnp.sum(home_grads, axis=(0, 2), dtype=jnp.float32)
    pixel_grads = jnp.einsum(
        "gvpd,vcd->gvcp", home_grads, emb_weight, preferred_element_type=jnp.float32
    )
    pixel_grads = pixel_grads.astype(jnp.bfloat16)
    emb_grad, var_embed_grad = lax.psum((table_part, offset_part), "item")
    (
        share_query,
        share_key,
        share_value,
        share_out,
        share_ln1_gain,
        share_ln1_bias,
        share_qkv,
        share_proj,
        share_ln2_gain,
        share_ln2_bias,
        share_fc1,
        share_fc1_bias,
        share_fc2,
        share_fc2_bias,
    ) = (
        lax.psum_scatter(agg_query_grad, "var", scatter_dimension=0, tiled=True),
        lax.psum_scatter(agg_key_grad, "var", scatter_dimension=1, tiled=True),
        lax.psum_scatter(agg_value_grad, "var", scatter_dimension=1, tiled=True),
        lax.psum_scatter(agg_out_grad, "var", scatter_dimension=1, tiled=True),
        lax.psum_scatter(ln1_gain_grad, "var", scatter_dimension=0, tiled=True),
        lax.psum_scatter(ln1_bias_grad, "var", scatter_dimension=0, tiled=True),
        lax.psum_scatter(qkv_grad, "var", scatter_dimension=1, tiled=True),
        lax.psum_scatter(proj_grad, "var", scatter_dimension=1, tiled=True),
        lax.psum_scatter(ln2_gain_grad, "var", scatter_dimension=0, tiled=True),
        lax.psum_scatter(ln2_bias_grad, "var", scatter_dimension=0, tiled=True),
        lax.psum_scatter(fc1_grad, "var", scatter_dimension=1, tiled=True),
        lax.psum_scatter(fc1_bias_grad, "var", scatter_dimension=0, tiled=True),
        lax.psum_scatter(fc2_grad, "var", scatter_dimension=1, tiled=True),
        lax.psum_scatter(fc2_bias_grad, "var", scatter_dimension=0, tiled=True),
    )
    summed_grads = lax.psum(
        (
            share_query,
            share_key,
            share_value,
            share_out,
            share_ln1_gain,
            share_ln1_bias,
            share_qkv,
            share_proj,
            share_ln2_gain,
            share_ln2_bias,
            share_fc1,
            share_fc1_bias,
            share_fc2,
            share_fc2_bias,
        ),
        "item",
    )
    output_rows = block_out.reshape(groups, patch_share, D).astype(jnp.bfloat16)
    return (output_rows, pixel_grads, emb_grad, var_embed_grad) + tuple(summed_grads)


def solution(mesh):
    in_specs = (
        P("item", "var", None, None),
        P("item"),
        P(),
        P(),
        P("var", None, None),
        P("var", None),
        P(),
        P(),
        P(),
        P(),
        P(),
        P(),
        P(),
        P(),
        P(),
        P(),
        P(),
        P(),
        P(),
        P(),
        P("item", "var", None),
    )
    out_specs = (
        P("item", "var", None),
        P("item", "var", None, None),
        P("var", None, None),
        P("var", None),
        P("var"),
        P(None, "var"),
        P(None, "var"),
        P(None, "var"),
        P("var"),
        P("var"),
        P(None, "var"),
        P(None, "var"),
        P("var"),
        P("var"),
        P(None, "var"),
        P("var"),
        P(None, "var"),
        P("var"),
    )
    return jax.shard_map(body, mesh=mesh, in_specs=in_specs, out_specs=out_specs, check_vma=False)
```

profile of v0, /device:TPU:0, one launch (start us, length us, event | category | flops | bytes accessed | tf_op | source)
XLA Modules:
  0.0 2123.2 jit_solution(1896602693328048025)
XLA Ops:
  8.1 15.5 fusion.2
  23.6 46.6 %copy.113 = bf16[1,8,2048,1024]{3,1,0,2:T(8,128)(2,1)} copy(bf16[1,8,2048,1024]{2,3,1,0:T(8,128)(2,1)} %fusion.2) | data formatting | bytes 67108864 | tf_op jit(solution)/shard_map/convert_element_type | solution.py:33
  70.2 7.2 all-to-all-start
  89.3 352.4 %all-to-all-done = bf16[1,8,2048,1024]{3,1,0,2:T(8,128)(2,1)} async-done(((bf16[1,8,2048,1024]{3,1,0,2:T(8,128)(2,1)}), bf16[1,8,2048,1024]{3,1,0,2:T(8,128)(2,1)}, u32[]{:S(2)}, u32[]{:S(2)}) %all-to-all-start) | async-done | bytes 33554464 | tf_op jit(solution)/shard_map/all_to_all | solution.py:137
  441.8 30.8 %copy.114 = bf16[1,8,8,256,1024]{4,3,1,2,0:T(8,128)(2,1)} copy(bf16[1,8,8,256,1024]{4,1,3,2,0:T(8,128)(2,1)} %bitcast.6) | data formatting | bytes 67108864 | tf_op jit(solution)/shard_map/all_to_all | solution.py:137
  472.6 15.0 fusion.188
  492.9 52.0 %fusion.16 = bf16[256,16,1024]{2,1,0:T(8,128)(2,1)S(1)} fusion(bf16[64,256,16]{0,2,1:T(8,128)(2,1)S(1)} %copy.116, bf16[64,256,1024]{2,1,0:T(8,128)(2,1)} %bitcast.396), kind=kOutput, calls=%fused_computation.35 | convolution fusion | flops 541065216 | bytes 42467328 | tf_op jit(solution)/shard_map/gvsh,gvsd->gshd/dot_general | solution.py:47
  567.7 27.7 %all-gather.8.cloned.1.call-done = bf16[1,2048,1024]{2,1,0:T(8,128)(2,1)} async-done(((bf16[1,256,1024]{2,1,0:T(8,128)(2,1)}), bf16[1,2048,1024]{2,1,0:T(8,128)(2,1)}) %all-gather.8.cloned.1.call-update) | async-done | bytes 4194320 | tf_op jit(solution)/shard_map/all_gather | solution.py:220
  629.2 22.3 %all-gather.6.cloned.1.call-done = bf16[1,2048,2048]{2,1,0:T(8,128)(2,1)} async-done(((bf16[1,256,2048]{2,1,0:T(8,128)(2,1)}), bf16[1,2048,2048]{2,1,0:T(8,128)(2,1)}) %all-gather.6.cloned.1.call-update) | async-done | bytes 8388624 | tf_op jit(solution)/shard_map/all_gather | solution.py:166
  670.8 18.0 multiply_reduce_fusion
  688.8 14.0 fusion.8
  702.8 16.5 fusion.190
  721.5 15.8 multiply_convert_fusion.8
  737.3 11.6 convert_reduce_fusion.1
  748.8 7.4 multiply_reduce_fusion.1
  804.2 7.1 reshape.700
  821.4 7.1 reshape.703
  838.5 7.5 reshape.706
  857.8 9.3 all-gather.1
  867.3 8.9 all_gather.17
  900.5 8.1 fusion.46
  908.6 8.1 fusion.99
  916.7 8.6 fusion.98
  925.3 6.9 fusion.105
  978.8 7.9 fusion.89
  986.7 7.9 fusion.91
  994.6 7.9 fusion.93
  1002.5 7.9 fusion.95
  1023.1 14.6 fusion.12
  1054.6 35.0 %fusion.4 = f32[256,64,16]{1,2,0:T(8,128)} fusion(bf16[64,256,1024]{2,1,0:T(8,128)(2,1)} %bitcast.397, bf16[256,16,1024]{2,0,1:T(8,128)(2,1)S(1)} %convert_bitcast_fusion), kind=kOutput, calls=%fused_computation.10 | convolution fusion | flops 536870912 | bytes 42991616 | tf_op jit(solution)/shard_map/while/body/eval_jaxpr/shd,vsd->vsh/dot_general | solution.py:54
  1093.1 13.4 fusion.108
  1111.6 8.6 fusion.173
  1121.4 9.7 fusion.137
  1133.5 24.9 %fusion.145 = f32[64,256,1024]{2,0,1:T(8,128)} fusion(bf16[64,256,16]{0,2,1:T(8,128)(2,1)S(1)} %copy.164, bf16[1024,16]{0,1:T(8,128)(2,1)S(1)} %copy-done.67), kind=kOutput, calls=%fused_computation.186 | convolution fusion | flops 536870912 | bytes 67665920 | tf_op jit(solution)/shard_map/while/body/eval_jaxpr/vsh,hd->vsd/dot_general | solution.py:62
  1158.4 42.8 %fusion.3 = bf16[1,64,256,1024]{3,1,2,0:T(8,128)(2,1)} fusion(f32[64,256,1024]{2,0,1:T(8,128)} %fusion.145, bf16[64,256,16]{0,2,1:T(8,128)(2,1)S(1)} %copy-done.15, bf16[256,16,1024]{2,0,1:T(8,128)(2,1)} %copy-done.3), kind=kOutput, calls=%fused_computation.6 | convolution fusion | flops 587202560 | bytes 109576192 | tf_op jit(solution)/shard_map/while/body/eval_jaxpr/vsh,shd->vsd/dot_general | solution.py:57
  1201.2 30.8 %copy.157 = bf16[1,64,256,1024]{3,2,0,1:T(8,128)(2,1)} copy(bf16[1,64,256,1024]{3,1,2,0:T(8,128)(2,1)} %fusion.3) | data formatting | bytes 67108864 | tf_op jit(solution)/shard_map/while/body/jit(dynamic_update_index_in_dim)/broadcast_in_dim | solution.py:276
  1232.1 7.6 all-to-all-start.1
  1240.0 6.9 fusion.132
  1247.0 491.2 %all-to-all-done.1 = bf16[1,64,256,1024]{3,2,0,1:T(8,128)(2,1)} async-done(((bf16[1,64,256,1024]{3,2,0,1:T(8,128)(2,1)}), bf16[1,64,256,1024]{3,2,0,1:T(8,128)(2,1)}, u32[]{:S(2)}, u32[]{:S(2)}) %all-to-all-start.1) | async-done | bytes 33554464 | tf_op jit(solution)/shard_map/all_to_all | solution.py:281
  1738.2 24.9 %copy.158 = bf16[1,8,8,256,1024]{4,3,1,2,0:T(8,128)(2,1)} copy(bf16[1,8,8,256,1024]{4,3,2,1,0:T(8,128)(2,1)} %bitcast.103) | data formatting | bytes 67108864 | tf_op jit(solution)/shard_map/all_to_all | solution.py:281
  1763.1 13.9 convolution_bitcast_fusion
  1777.2 43.1 %reduce-scatter.14.cloned.1.call-done = f32[1024,384]{1,0:T(8,128)} async-done(((f32[1024,3072]{1,0:T(8,128)}), f32[1024,384]{1,0:T(8,128)}) %reduce-scatter.14.cloned.1.call-update) | async-done | bytes 1572880 | tf_op jit(solution)/shard_map/reduce_scatter | solution.py:313
  1822.3 7.2 fusion.107
  1829.5 25.0 %all-reduce.7 = (f32[1024]{0:T(1024)S(1)}, f32[1024]{0:T(1024)S(1)}, f32[1024]{0:T(1024)S(1)}, f32[1024]{0:T(1024)S(1)}, f32[1024]{0:T(1024)S(1)}, /*index=5*/f32[4096]{0:T(1024)S(1)}, f32[1024]{0:T(1024)S(1)}) all-reduce(f32[1024]{0:T(1024)S(1)} %copy-done.92, ...), channel_id=4, replica_groups=mesh['item'=4,'var'=8] {'var'}, use_global_device_ids=true, to_apply=%region_20.21.clone | all-reduce | flops 10240 | bytes 81920
  1855.0 11.7 convert_reduce_fusion
  1866.7 22.5 %all-reduce.8 = (f32[8,1024]{1,0:T(8,128)}, f32[128]{0:T(128)}, f32[128]{0:T(128)}, f32[128]{0:T(128)}, f32[128]{0:T(128)}, /*index=5*/f32[128]{0:T(128)}, f32[512]{0:T(512)}, f32[128]{0:T(128)}) all-reduce(f32[8,1024]{1,0:T(8,128)S(1)} %convert_reduce_fusion, f32[128]{0:T(128)S(1)} %dynamic-slice.1, ...), channel_id=1, replica_groups=mesh['item'=4,'var'=8] {'item'}, use_global_device_ids=true, to_apply=%region_18.19 | all-reduce | flops 9472 | bytes 75776 | tf_op jit(solution)/shard_map/psum | solution.py:290
  1889.2 15.0 fusion.71
  1904.2 200.0 %all-reduce.12.cloned.1.call-done = (f32[8,4,1024]{2,1,0:T(4,128)}, f32[1024,128]{0,1:T(8,128)}, f32[1024,128]{1,0:T(8,128)}, f32[1024,128]{1,0:T(8,128)}, f32[1...) async-done(((f32[8,4,1024]{2,1,0:T(4,128)}, f32[1024,128]{0,1:T(8,128)}, f32[1024,128]{1,0:T(8,128)}, f32[1024,128]{1,0:T(8,128)}, ...) | async-done | bytes 7995408 | tf_op jit(solution)/shard_map/psum | solution.py:290
  (389 shorter events, 299.3 us)
Async XLA Ops:
  7.2 712.1 %copy-start = (bf16[1024,1024]{1,0:T(8,128)(2,1)S(1)}, bf16[1024,1024]{1,0:T(8,128)(2,1)}, u32[]{:S(2)}) copy-start(bf16[1024,1024]{1,0:T(8,128)(2,1)} %param.34) | copy-start | bytes 6291460
  70.2 371.5 %all-to-all-start = ((bf16[1,8,2048,1024]{3,1,0,2:T(8,128)(2,1)}), bf16[1,8,2048,1024]{3,1,0,2:T(8,128)(2,1)}, u32[]{:S(2)}, u32[]{:S(2)}) async-start(bf16[1,8,2048,1024]{3,1,0,2:T(8,128)(2,1)} %copy.113), calls=%async_computation | async-start | bytes 67108864 | tf_op jit(solution)/shard_map/all_to_all | solution.py:137
  77.5 9.2 copy-start.104
  77.5 9.2 copy-start.105
  77.5 517.9 %all-gather.8.cloned.1.call-start = ((), (), s32[]{:S(2)}) async-start(), calls=%async_computation.10 | async-start | bytes 4718592 | tf_op jit(solution)/shard_map/all_gather | solution.py:220
  82.0 390.5 %copy-start.79 = (f32[1024]{0:T(1024)}, f32[1024]{0:T(1024)S(1)}, u32[]{:S(2)}) copy-start(f32[1024]{0:T(1024)S(1)} %convert_element_type.222) | copy-start | bytes 12292
  86.7 465.0 %copy-start.74 = (f32[1024]{0:T(1024)}, f32[1024]{0:T(1024)S(1)}, u32[]{:S(2)}) copy-start(f32[1024]{0:T(1024)S(1)} %convert_element_type.230) | copy-start | bytes 12292
  86.7 465.0 %copy-start.77 = (f32[1024]{0:T(1024)}, f32[1024]{0:T(1024)S(1)}, u32[]{:S(2)}) copy-start(f32[1024]{0:T(1024)S(1)} %convert_element_type.231) | copy-start | bytes 12292
  89.2 383.4 %copy-start.66 = (bf16[1024,16]{0,1:T(8,128)(2,1)}, bf16[1024,16]{0,1:T(8,128)(2,1)S(1)}, u32[]{:S(2)}) copy-start(bf16[1024,16]{0,1:T(8,128)(2,1)S(1)} %bitcast_reduce_fusion) | copy-start | bytes 98308
  89.3 398.5 %copy-start.96 = (f32[64]{0:T(128)}, f32[64]{0:T(128)S(1)}, u32[]{:S(2)}) copy-start(f32[64]{0:T(128)S(1)} %get-tuple-element.150) | copy-start | bytes 772
  492.9 52.1 %copy-start.14 = (bf16[64,256,16]{0,2,1:T(8,128)(2,1)}, bf16[64,256,16]{0,2,1:T(8,128)(2,1)S(1)}, u32[]{:S(2)}) copy-start(bf16[64,256,16]{0,2,1:T(8,128)(2,1)S(1)} %copy.116) | copy-start | bytes 1572868
  492.9 52.1 %copy-start.19 = (bf16[1024,1024]{0,1:T(8,128)(2,1)S(1)}, bf16[1024,1024]{0,1:T(8,128)(2,1)}, u32[]{:S(2)}) copy-start(bf16[1024,1024]{0,1:T(8,128)(2,1)} %copy.118) | copy-start | bytes 6291460
  550.7 168.6 %copy-start.6 = (f32[256,1024]{1,0:T(8,128)}, f32[256,1024]{1,0:T(8,128)S(1)}, u32[]{:S(2)}) copy-start(f32[256,1024]{1,0:T(8,128)S(1)} %get-tuple-element.154) | copy-start | bytes 3145732
  558.4 93.2 %all-gather.6.cloned.1.call-start = ((), (), s32[]{:S(2)}) async-start(), calls=%async_computation.9 | async-start | bytes 9437184 | tf_op jit(solution)/shard_map/all_gather | solution.py:166
  560.9 371.3 %all-gather.10.cloned.1.call-start = ((), (), s32[]{:S(2)}) async-start(), calls=%async_computation.18 | async-start | bytes 4718592 | tf_op jit(solution)/shard_map/all_gather | solution.py:221
  561.0 195.3 %copy-start.70 = (f32[1024]{0:T(1024)}, f32[1024]{0:T(1024)S(1)}, u32[]{:S(2)}) copy-start(f32[1024]{0:T(1024)S(1)} %convert_element_type.236) | copy-start | bytes 12292
  561.0 160.5 %copy-start.72 = (f32[1024]{0:T(1024)}, f32[1024]{0:T(1024)S(1)}, u32[]{:S(2)}) copy-start(f32[1024]{0:T(1024)S(1)} %convert_element_type.237) | copy-start | bytes 12292
  721.2 35.1 %copy-start.11 = (f32[256,1024]{1,0:T(8,128)}, f32[256,1024]{1,0:T(8,128)S(1)}, u32[]{:S(2)}) copy-start(f32[256,1024]{1,0:T(8,128)S(1)} %get-tuple-element.160) | copy-start | bytes 3145732
  721.2 35.1 %copy-start.81 = (f32[256]{0:T(256)}, f32[256]{0:T(256)S(1)}, u32[]{:S(2)}) copy-start(f32[256]{0:T(256)S(1)} %broadcast_multiply_fusion) | copy-start | bytes 3076
  721.5 34.8 %copy-start.86 = (f32[256]{0:T(256)}, f32[256]{0:T(256)S(1)}, u32[]{:S(2)}) copy-start(f32[256]{0:T(256)S(1)} %fusion.155) | copy-start | bytes 3076
  721.5 15.8 copy-start.24
  761.0 1016.0 %reduce-scatter.16.cloned.1.call-start = ((), (), s32[]{:S(2)}) async-start(), calls=%async_computation.15 | async-start | bytes 4718592 | tf_op jit(solution)/shard_map/reduce_scatter | solution.py:314
  856.0 20.8 copy-start.46
  899.5 877.5 %reduce-scatter.10.cloned.1.call-start = ((), (), s32[]{:S(2)}) async-start(), calls=%async_computation.12 | async-start | bytes 4718592 | tf_op jit(solution)/shard_map/reduce_scatter | solution.py:309
  908.6 8.1 copy-start.39
  916.7 8.6 copy-start.41
  964.5 11.1 slice-start
  1043.1 733.9 %reduce-scatter.12.cloned.1.call-start = ((), (), s32[]{:S(2)}) async-start(), calls=%async_computation.13 | async-start | bytes 4718592 | tf_op jit(solution)/shard_map/reduce_scatter | solution.py:310
  1046.9 730.2 %reduce-scatter.8.cloned.1.call-start = ((), (), s32[]{:S(2)}) async-start(), calls=%async_computation.11 | async-start | bytes 4718592 | tf_op jit(solution)/shard_map/reduce_scatter | solution.py:308
  1054.6 37.9 %copy-start.5 = (f32[64,256,16]{1,2,0:T(8,128)S(1)}, f32[64,256,16]{1,2,0:T(8,128)}, u32[]{:S(2)}) copy-start(f32[64,256,16]{1,2,0:T(8,128)} %copy-done.4) | copy-start | bytes 3145732
  1054.6 37.9 %copy-start.64 = (f32[256,16]{0,1:T(8,128)S(1)}, f32[256,16]{0,1:T(8,128)}, u32[]{:S(2)}) copy-start(f32[256,16]{0,1:T(8,128)} %copy-done.63) | copy-start | bytes 49156
  1054.6 37.9 %copy-start.69 = (f32[256,16]{0,1:T(8,128)S(1)}, f32[256,16]{0,1:T(8,128)}, u32[]{:S(2)}) copy-start(f32[256,16]{0,1:T(8,128)} %copy-done.68) | copy-start | bytes 49156
  1054.6 37.9 %copy-start.97 = (f32[64]{0:T(128)S(1)}, f32[64]{0:T(128)}, u32[]{:S(2)}) copy-start(f32[64]{0:T(128)} %copy-done.96) | copy-start | bytes 772
  1093.1 13.5 copy-start.21
  1093.1 13.5 copy-start.10
  1093.1 13.5 copy-start.80
  1110.0 667.2 %reduce-scatter.18.cloned.1.call-start = ((), (), s32[]{:S(2)}) async-start(), calls=%async_computation.16 | async-start | bytes 18874368 | tf_op jit(solution)/shard_map/reduce_scatter | solution.py:317
  1120.3 656.8 %reduce-scatter.20.cloned.1.call-start = ((), (), s32[]{:S(2)}) async-start(), calls=%async_computation.17 | async-start | bytes 18874368 | tf_op jit(solution)/shard_map/reduce_scatter | solution.py:319
  1133.5 24.9 %copy-start.15 = (bf16[64,256,16]{0,2,1:T(8,128)(2,1)S(1)}, bf16[64,256,16]{0,2,1:T(8,128)(2,1)}, u32[]{:S(2)}) copy-start(bf16[64,256,16]{0,2,1:T(8,128)(2,1)} %copy-done.14) | copy-start | bytes 1572868
  1232.1 506.1 %all-to-all-start.1 = ((bf16[1,64,256,1024]{3,2,0,1:T(8,128)(2,1)}), bf16[1,64,256,1024]{3,2,0,1:T(8,128)(2,1)}, u32[]{:S(2)}, u32[]{:S(2)}) async-start(bf16[1,64,256,1024]{3,2,0,1:T(8,128)(2,1)} %copy.157), calls=%async_computation.1 | async-start | bytes 67108864 | tf_op jit(solution)/shard_map/all_to_all | solution.py:281
  1239.7 580.6 %reduce-scatter.14.cloned.1.call-start = ((), (), s32[]{:S(2)}) async-start(), calls=%async_computation.14 | async-start | bytes 14155776 | tf_op jit(solution)/shard_map/reduce_scatter | solution.py:313
  1246.9 857.2 %all-reduce.12.cloned.1.call-start = ((), (), s32[]{:S(2)}) async-start(), calls=%async_computation.19 | async-start | bytes 15990784 | tf_op jit(solution)/shard_map/psum | solution.py:290
  1738.2 24.9 %copy-start.58 = (bf16[1,8,4,2048]{3,2,1,0:T(4,128)(2,1)S(1)}, bf16[1,8,4,2048]{3,2,1,0:T(4,128)(2,1)}, u32[]{:S(2)}) copy-start(bf16[1,8,4,2048]{3,2,1,0:T(4,128)(2,1)} %param.21) | copy-start | bytes 393220
  1777.0 43.3 %copy-start.111 = (u32[32]{0:T(128)S(1)}, u32[32]{0:T(128)}, u32[]{:S(2)}) copy-start(u32[32]{0:T(128)} %constant.122) | copy-start | bytes 388
  1777.0 45.2 %copy-start.108 = (bf16[1024]{0:T(1024)(128)(2,1)S(1)}, bf16[1024]{0:T(1024)(128)(2,1)}, u32[]{:S(2)}) copy-start(bf16[1024]{0:T(1024)(128)(2,1)} %param.40) | copy-start | bytes 6148
  1777.0 45.2 %copy-start.13 = (f32[256,1024]{1,0:T(8,128)S(1)}, f32[256,1024]{1,0:T(8,128)}, u32[]{:S(2)}) copy-start(f32[256,1024]{1,0:T(8,128)} %copy-done.11) | copy-start | bytes 3145732
  1855.0 34.2 %copy-start.65 = (bf16[8,4,1024]{2,1,0:T(4,128)(2,1)S(1)}, bf16[8,4,1024]{2,1,0:T(4,128)(2,1)}, u32[]{:S(2)}) copy-start(bf16[8,4,1024]{2,1,0:T(4,128)(2,1)} %param.25) | copy-start | bytes 196612
  2104.2 8.8 copy-start.62
  (79 other events, 375.1 us)
Sparse Core Ops, SparseCore 0:
  558.5 36.8 all-gather.7
  597.3 54.2 all-gather.5
  761.1 36.5 all-gather.9
  899.6 51.0 reduce-scatter.15
  1043.3 51.3 reduce-scatter.9
  1097.9 51.0 reduce-scatter.11
  1152.3 51.1 reduce-scatter.7
  1207.1 307.7 reduce-scatter.17
  1518.5 207.3 reduce-scatter.19
  1729.2 91.0 reduce-scatter.13
  1824.3 279.7 all-reduce.11
where the time goes:
time: 2130 us; the launch traced here: 2120 us
  waiting for transfers between devices  1140 us (54%)
  matrix products  495 us (23%)
  local copies, waits for them, and re-layouts  347 us (16%)
  blocking collectives  65.6 us (3%)
  other arithmetic  42.9 us (2%)
    all_to_all x1, waiting for transfers between devices, body(): lax.all_to_all(g_tokens, 'var', split_axis=1, concat_axis=2, tiled=True)  491 us
    all_to_all x1, waiting for transfers between devices, body(): lax.all_to_all(local_tokens, 'var', split_axis=2, concat_axis=1, tiled=True)  352 us
    psum x1, waiting for transfers between devices, body(): emb_grad, var_embed_grad = lax.psum((table_part, offset_part), 'item')  200 us
    unnamed x256, local copies, waits for them, and re-layouts  61.4 us
    dot_general x1, matrix products, aggregate_forward(): jnp.einsum('gvsh,gvsd->gshd', weights_low, tokens, preferred_element_type...  52 us
    another operation x16, local copies, waits for them, and re-layouts  51.5 us
    convert_element_type x1, local copies, waits for them, and re-layouts, embed_tokens(): (spread + offsets.astype(jnp.float32)[None, :, None, :]).astype(jnp.bfloa...  46.6 us
    reduce_scatter x1, waiting for transfers between devices, body(): lax.psum_scatter(qkv_grad, 'var', scatter_dimension=1, tiled=True)  43.1 us
  transfers between devices with their start and end apart: 13, of which 6 were waited for; matrix products, arithmetic and copies ran while one was open for 27% of the time, Pallas kernels for 0%

commit v1 on v0

v1 whole, which is shorter than its diff:
```python
import jax
import jax.numpy as jnp
from jax import lax
from jax.sharding import PartitionSpec as P

D = 1024
HEADS = 16
HEAD_DIM = 64
PATCHES = 2048
NDATA = 5
PRECISE = lax.Precision.HIGHEST
FACTOR = HEAD_DIM ** (-0.5)
F32 = jnp.float32
BF16 = jnp.bfloat16


def mm(spec, a, b):
    return jnp.einsum(spec, a, b, preferred_element_type=F32)


def norm_stats(values):
    center = values - jnp.mean(values, axis=-1, keepdims=True)
    spread = jnp.mean(center * center, axis=-1, keepdims=True)
    inv = lax.rsqrt(spread + 1e-06)
    return center * inv, inv


def norm_back(grad, gain_vec, normed, inv):
    u = grad * gain_vec
    mean_u = jnp.mean(u, axis=-1, keepdims=True)
    mean_un = jnp.mean(u * normed, axis=-1, keepdims=True)
    return inv * (u - mean_u - normed * mean_un)


def listed(array, axis):
    shape = array.shape
    split = shape[:axis] + (shape[axis] // 4, 4) + shape[axis + 1 :]
    kept = lax.slice_in_dim(array.reshape(split), 0, 3, axis=axis + 1)
    return kept.reshape(shape[:axis] + (shape[axis] // 4 * 3,) + shape[axis + 1 :])


def unlisted(array, axis):
    shape = array.shape
    split = shape[:axis] + (shape[axis] // 3, 3) + shape[axis + 1 :]
    pads = [(0, 0)] * len(split)
    pads[axis + 1] = (0, 1)
    full = jnp.pad(array.reshape(split), pads)
    return full.reshape(shape[:axis] + (shape[axis] // 3 * 4,) + shape[axis + 1 :])


def to_heads(rows, lanes, parts):
    g, r, _ = rows.shape
    wide = rows.reshape(g, r, parts, lanes, D // lanes)
    out = lax.all_to_all(wide, "var", split_axis=3, concat_axis=1, tiled=True)
    return out.reshape(g, r * lanes, parts, D // lanes)


def from_heads(cols, lanes):
    g, p, parts, w = cols.shape
    out = lax.all_to_all(
        cols.reshape(g, p, parts, 1, w), "var", split_axis=1, concat_axis=3, tiled=True
    )
    return out.reshape(g, p // lanes, parts * w * lanes)


def attention_forward(queries, keys, values):
    scores = mm("gshe,gkhe->ghsk", queries, keys) * FACTOR
    highest = jnp.max(scores, axis=-1, keepdims=True)
    terms = jnp.exp(scores - highest)
    totals = jnp.sum(terms, axis=-1, keepdims=True)
    attended = mm("ghsk,gkhe->gshe", (terms / totals).astype(BF16), values)
    return attended, highest + jnp.log(totals)


def attention_back(queries, keys, values, g_att, lse, rowdot):
    probs = jnp.exp(mm("gshe,gkhe->ghsk", queries, keys) * FACTOR - lse)
    g_probs = mm("gshe,gkhe->ghsk", g_att, values)
    g_scores = (probs * (g_probs - rowdot)).astype(BF16)
    g_q = mm("ghsk,gkhe->gshe", g_scores, keys) * FACTOR
    g_k = mm("ghsk,gshe->gkhe", g_scores, queries) * FACTOR
    g_v = mm("ghsk,gshe->gkhe", probs.astype(BF16), g_att)
    return g_q, g_k, g_v


def body(
    pixels,
    dataset,
    var_mask,
    data_weight,
    emb_weight,
    var_embed,
    agg_query,
    agg_key,
    agg_value,
    agg_out,
    ln1_gain,
    ln1_bias,
    qkv_weight,
    proj_weight,
    ln2_gain,
    ln2_bias,
    fc1_weight,
    fc1_bias,
    fc2_weight,
    fc2_bias,
    cotangent,
):
    g = pixels.shape[0]
    slots = var_mask.shape[1]
    pix = pixels.shape[2]
    lanes = lax.axis_size("var")
    own_slots = slots // lanes
    mine = lax.axis_index("var")
    r = PATCHES // lanes
    rows = g * r
    live = slots // 4 * 3
    hot = (dataset[:, None] == jnp.arange(NDATA, dtype=jnp.int32)[None, :]).astype(F32)
    counts = data_weight.astype(F32)
    item_scale = jnp.dot(hot, counts, precision=PRECISE) * NDATA / jnp.sum(counts)
    mask = listed(jnp.dot(hot, var_mask.astype(F32), precision=PRECISE), 1)

    own_table = jnp.concatenate([emb_weight, var_embed[:, None, :]], axis=1)
    table = lax.all_gather(own_table, "var", axis=0, tiled=True)
    table = jnp.transpose(listed(table, 0), (1, 0, 2))
    flat_table = table.reshape((pix + 1) * live, D)
    patch_pix = lax.all_to_all(pixels, "var", split_axis=3, concat_axis=1, tiled=True)
    patch_pix = jnp.transpose(listed(patch_pix, 1), (0, 2, 1, 3))
    xs = jnp.concatenate([patch_pix, jnp.ones((g, 1, live, r), BF16)], axis=1)

    query_full = agg_query.astype(F32)
    key_full = agg_key.astype(F32)
    probe = (key_full * query_full[None, :]).reshape(D, HEADS, HEAD_DIM).sum(axis=-1)
    probe = probe.T.astype(BF16)
    seen = mm("xd,hd->hx", flat_table, probe).reshape(HEADS, pix + 1, live) * FACTOR
    ev = mm("xd,de->xe", flat_table, agg_value).astype(BF16)
    ev_heads = ev.reshape(pix + 1, live, HEADS, HEAD_DIM)

    xf = xs.astype(F32)
    scores = sum(seen[None, :, c, :, None] * xf[:, None, c] for c in range(pix + 1))
    present = mask[:, None, :, None]
    scores = jnp.where(present > 0.5, scores, -1e30)
    highest = jnp.max(scores, axis=2, keepdims=True)
    terms = jnp.exp(scores - highest) * present
    weights = terms / jnp.sum(terms, axis=2, keepdims=True)
    low = weights.astype(BF16)
    wx = low[:, :, None] * xs[:, None]
    mixed = mm("ghcvr,cvhe->grhe", wx, ev_heads).astype(BF16).reshape(rows, D)
    result = jnp.dot(mixed, agg_out, preferred_element_type=F32)

    vectors = [v.astype(F32) for v in (ln1_gain, ln1_bias, ln2_gain, ln2_bias, fc1_bias, fc2_bias)]
    gain1, shift1, gain2, shift2, bias1, bias2 = vectors
    normed1, inv1 = norm_stats(result)
    first = (normed1 * gain1 + shift1).astype(BF16)
    qkv = jnp.dot(first, qkv_weight, preferred_element_type=F32).astype(BF16).reshape(g, r, 3 * D)

    by_head = HEADS % lanes == 0
    if by_head:
        own_heads = HEADS // lanes
        heads = to_heads(qkv, lanes, 3).reshape(g, PATCHES, 3, own_heads, HEAD_DIM)
        queries, keys, values = heads[:, :, 0], heads[:, :, 1], heads[:, :, 2]
    else:
        queries = qkv[..., :D].reshape(g, r, HEADS, HEAD_DIM)
        pair = lax.all_gather(qkv[..., D:], "var", axis=1, tiled=True)
        pair = pair.reshape(g, PATCHES, 2, HEADS, HEAD_DIM)
        keys, values = pair[:, :, 0], pair[:, :, 1]
    att_full, lse = attention_forward(queries, keys, values)
    att = att_full.astype(BF16).reshape(g, att_full.shape[1], -1)
    if by_head:
        attended = from_heads(att[:, :, None, :], lanes).reshape(rows, D)
    else:
        attended = att.reshape(rows, D)

    residual = result + jnp.dot(attended, proj_weight, preferred_element_type=F32)
    normed2, inv2 = norm_stats(residual)
    second = (normed2 * gain2 + shift2).astype(BF16)
    pre = jnp.dot(second, fc1_weight, preferred_element_type=F32) + bias1
    cdf = 0.5 * (1.0 + lax.erf(pre * (0.5**0.5)))
    slope = cdf + pre * jnp.exp(-0.5 * pre * pre) * 0.3989422804014327
    act = (pre * cdf).astype(BF16)
    block_out = residual + jnp.dot(act, fc2_weight, preferred_element_type=F32) + bias2

    g_final = (cotangent.astype(F32) * item_scale[:, None, None]).reshape(rows, D)
    g_mlp = g_final.astype(BF16)
    fc2_t = mm("rd,rf->df", g_mlp, act).astype(BF16)
    g_pre = (mm("rd,fd->rf", g_mlp, fc2_weight) * slope).astype(BF16)
    fc1_t = mm("rf,rd->fd", g_pre, second).astype(BF16)
    g_second = mm("rf,df->rd", g_pre, fc1_weight)
    g_resid = g_final + norm_back(g_second, gain2, normed2, inv2)
    g_branch = g_resid.astype(BF16)
    proj_t = mm("re,rd->ed", g_branch, attended).astype(BF16)
    g_att = mm("re,de->rd", g_branch, proj_weight).astype(BF16).reshape(g, r, D)
    if by_head:
        g_att = to_heads(g_att, lanes, 1)
    g_att = g_att.reshape(att_full.shape)
    rowdot = jnp.transpose(jnp.sum(g_att.astype(F32) * att_full, axis=-1), (0, 2, 1))[..., None]
    g_q, g_k, g_v = attention_back(queries, keys, values, g_att, lse, rowdot)
    if by_head:
        width = D // lanes
        parts = [t.astype(BF16).reshape(g, PATCHES, 1, width) for t in (g_q, g_k, g_v)]
        g_qkv = from_heads(jnp.concatenate(parts, axis=2), lanes)
    else:
        parts = [
            lax.psum_scatter(t, "var", scatter_dimension=1, tiled=True).reshape(g, r, D)
            for t in (g_k, g_v)
        ]
        g_qkv = jnp.concatenate([g_q.reshape(g, r, D)] + parts, axis=-1).astype(BF16)
    g_qkv = g_qkv.reshape(rows, 3 * D)
    qkv_t = mm("re,rd->ed", g_qkv, first).astype(BF16)
    g_first = mm("re,de->rd", g_qkv, qkv_weight)
    g_result = (g_resid + norm_back(g_first, gain1, normed1, inv1)).astype(BF16)
    out_t = mm("rd,rj->dj", g_result, mixed).astype(BF16)
    g_mixed = mm("rd,jd->rj", g_result, agg_out).astype(BF16).reshape(g, r, HEADS, HEAD_DIM)

    back = mm("cvhe,grhe->ghcvr", ev_heads, g_mixed)
    g_w = jnp.sum(back * xf[:, None], axis=2)
    rowsum = jnp.sum(weights * g_w, axis=2, keepdims=True)
    g_s = weights * (g_w - rowsum)
    pixel_grads = jnp.sum(low.astype(F32)[:, :, None] * back[:, :, :pix], axis=1)
    pixel_grads = pixel_grads + jnp.sum(
        g_s[:, :, None] * seen[None, :, :pix, :, None], axis=1
    )
    pixel_grads = unlisted(jnp.transpose(pixel_grads, (0, 2, 1, 3)).astype(BF16), 1)
    pixel_out = lax.all_to_all(pixel_grads, "var", split_axis=1, concat_axis=3, tiled=True)
    t_part = jnp.sum(g_s[:, :, None] * xf[:, None], axis=(0, 4))
    m_part = mm("ghcvr,grhe->cvhe", wx, g_mixed).reshape((pix + 1) * live, D)

    small = [
        jnp.sum(g_second * normed2, axis=0),
        jnp.sum(g_second, axis=0),
        jnp.sum(g_first * normed1, axis=0),
        jnp.sum(g_first, axis=0),
        jnp.sum(g_mlp.astype(F32), axis=0),
        jnp.sum(g_pre.astype(F32), axis=0),
        t_part.reshape(-1),
    ]
    sizes = [s.shape[0] for s in small]
    small_sum, m_sum = lax.psum((jnp.concatenate(small), m_part), ("item", "var"))
    ends = [sum(sizes[:k]) for k in range(len(sizes) + 1)]
    pieces = [small_sum[ends[k] : ends[k + 1]] for k in range(len(sizes))]

    def own(vector):
        width = vector.shape[0] // lanes
        return lax.dynamic_slice_in_dim(vector, mine * width, width)

    ln2_gain_grad, ln2_bias_grad, ln1_gain_grad, ln1_bias_grad, fc2_bias_grad, fc1_bias_grad = [
        own(p) for p in pieces[:6]
    ]
    t_sum = pieces[6].reshape(HEADS, (pix + 1) * live)

    m_slots = unlisted(m_sum.reshape(pix + 1, live, D), 1)
    t_slots = unlisted(t_sum.reshape(HEADS, pix + 1, live), 2)
    m_own = lax.dynamic_slice_in_dim(m_slots, mine * own_slots, own_slots, axis=1)
    t_own = lax.dynamic_slice_in_dim(t_slots, mine * own_slots, own_slots, axis=2)
    table_grad = mm("cve,de->vcd", m_own.astype(BF16), agg_value)
    table_grad = table_grad + jnp.einsum(
        "hcv,hd->vcd", t_own * FACTOR, probe.astype(F32), precision=PRECISE
    )
    width = D // lanes
    m_cols = lax.dynamic_slice_in_dim(m_sum, mine * width, width, axis=1)
    value_grad = mm("xd,xe->de", flat_table, m_cols.astype(BF16))
    g_probe = jnp.dot(t_sum, flat_table.astype(F32), precision=PRECISE) * FACTOR
    head_of = jnp.arange(D) // HEAD_DIM
    own_head = lax.dynamic_slice_in_dim(head_of, mine * width, width)
    pick = (own_head[None, :] == jnp.arange(HEADS)[:, None]).astype(F32)
    g_cols = jnp.einsum("hk,he->ke", g_probe, pick, precision=PRECISE)
    own_query = lax.dynamic_slice_in_dim(query_full, mine * width, width)
    own_key = lax.dynamic_slice_in_dim(agg_key, mine * width, width, axis=1).astype(F32)
    key_grad = g_cols * own_query[None, :]
    query_grad = jnp.sum(g_cols * own_key, axis=0)

    def reduced(grad):
        share = lax.psum_scatter(grad, "var", scatter_dimension=0, tiled=True)
        return lax.psum(share, "item").astype(F32).T

    fc2_grad, fc1_grad, proj_grad, qkv_grad, out_grad = [
        reduced(t) for t in (fc2_t, fc1_t, proj_t, qkv_t, out_t)
    ]
    return (
        block_out.reshape(g, r, D).astype(BF16),
        pixel_out,
        table_grad[:, :pix],
        table_grad[:, pix],
        query_grad,
        key_grad,
        value_grad,
        out_grad,
        ln1_gain_grad,
        ln1_bias_grad,
        qkv_grad,
        proj_grad,
        ln2_gain_grad,
        ln2_bias_grad,
        fc1_grad,
        fc1_bias_grad,
        fc2_grad,
        fc2_bias_grad,
    )


def solution(mesh):
    in_specs = (
        P("item", "var", None, None),
        P("item"),
        P(),
        P(),
        P("var", None, None),
        P("var", None),
        *([P()] * 14),
        P("item", "var", None),
    )
    cols = P(None, "var")
    vec = P("var")
    out_specs = (
        P("item", "var", None),
        P("item", "var", None, None),
        P("var", None, None),
        P("var", None),
        vec,
        cols,
        cols,
        cols,
        vec,
        vec,
        cols,
        cols,
        vec,
        vec,
        cols,
        vec,
        cols,
        vec,
    )
    return jax.shard_map(body, mesh=mesh, in_specs=in_specs, out_specs=out_specs, check_vma=False)
```

time: 2130 us -> 737 us (0.35)
  waiting for transfers between devices: 1140 us -> 272 us
  matrix products: 495 us -> 147 us
  local copies, waits for them, and re-layouts: 347 us -> 101 us
  blocking collectives: 65.6 us -> 122 us
    all_to_all x2 -> x4, waiting for transfers between devices: 844 us -> 13.8 us  [the longest x1 7.71 us: from_heads(): lax.all_to_all(cols.reshape(g, p, parts, 1, w), 'var', split_axis=1, conc...]
    dot_general x50 -> x29, matrix products: 495 us -> 145 us  [the longest x22 120 us: mm(): return jnp.einsum(spec, a, b, preferred_element_type=F32)]
    reduce_scatter x7 -> x5, waiting for transfers between devices: 43.2 us -> 210 us  [reduced(): share = lax.psum_scatter(grad, 'var', scatter_dimension=0, tiled=True)]
    psum x1, waiting for transfers between devices: 200 us -> 47.9 us  [reduced(): return lax.psum(share, 'item').astype(F32).T]
    slice x16 -> x10, local copies, waits for them, and re-layouts: 58.8 us -> 2.31 us  [the longest x3 1.37 us: body(): pieces = [small_sum[ends[k]:ends[k + 1]] for k in range(len(sizes))]]
    all_to_all x0 -> x2, blocking collectives: none -> 53.3 us  [the longest x1 29 us: from_heads(): lax.all_to_all(cols.reshape(g, p, parts, 1, w), 'var', split_axis=1, conc...]
    all_gather x3 -> x0, waiting for transfers between devices: 50.1 us -> none  [the longest x1 27.7 us: body(): lax.all_gather(queries.reshape(groups, patch_share, D), 'var', axis=1, ti...]
    convert_element_type x6 -> x4, local copies, waits for them, and re-layouts: 52.9 us -> 4.21 us  [the longest x2 3.95 us: body(): g_att.astype(F32) * att_full]
  transfers between devices with their start and end apart: 13 -> 10, of which waited for: 6 -> 6; matrix products, arithmetic and copies ran while one was open for 27% -> 21% of each run, Pallas kernels for 0% -> 0%
where the time goes in v1:
time: 737 us; the launch traced here: 726 us
  waiting for transfers between devices  272 us (37%)
  matrix products  147 us (20%)
  blocking collectives  122 us (17%)
  local copies, waits for them, and re-layouts  101 us (14%)
  other arithmetic  48.6 us (7%)
  between operations  18.2 us (2%)
  starting transfers between devices  16.9 us (2%)
    reduce_scatter x5, waiting for transfers between devices, reduced(): share = lax.psum_scatter(grad, 'var', scatter_dimension=0, tiled=True)  210 us
    dot_general x22, matrix products, mm(): return jnp.einsum(spec, a, b, preferred_element_type=F32)  120 us
    psum x1, blocking collectives, body(): lax.psum((jnp.concatenate(small), m_part), ('item', 'var'))  58.4 us
    psum x1, waiting for transfers between devices, reduced(): return lax.psum(share, 'item').astype(F32).T  47.9 us
    unnamed x215, local copies, waits for them, and re-layouts  46.7 us
    all_to_all x1, blocking collectives, from_heads(): lax.all_to_all(cols.reshape(g, p, parts, 1, w), 'var', split_axis=1, conc...  29 us
    all_to_all x1, blocking collectives, to_heads(): out = lax.all_to_all(wide, 'var', split_axis=3, concat_axis=1, tiled=True)  24.3 us
  transfers between devices with their start and end apart: 10, of which 6 were waited for; matrix products, arithmetic and copies ran while one was open for 21% of the time, Pallas kernels for 0%

profile of v1, /device:TPU:0, one launch (start us, length us, event | category | flops | bytes accessed | tf_op | source)
XLA Modules:
  0.0 726.5 jit_solution(15153634493656317930)
XLA Ops:
  7.2 4.0 copy.204
  11.3 4.0 reshape.523
  15.3 5.2 all-to-all-start
  20.5 3.9 copy.203
  24.5 10.6 %all_gather.3 = bf16[64,5,1024]{2,0,1:T(8,128)(2,1)S(1)} all-gather(bf16[8,5,1024]{2,0,1:T(8,128)(2,1)S(1)} %pad_maximum_fusion), channel_id=1, replica_groups=mesh['item'=4,'var'=8] {'var'}, dimensions={0}, use_global_device_ids=true | all-gather | bytes 737280 | tf_op jit(solution)/shard_map/all_gather | solution.py:123
  35.9 2.7 bitcast_reduce_fusion
  44.0 3.5 reshape.524
  47.4 3.2 copy.205
  56.6 4.7 fusion.26
  62.0 24.3 %all_to_all.93 = bf16[1,256,3,8,128]{4,1,2,0,3:T(8,128)(2,1)} all-to-all(bf16[1,256,3,8,128]{4,1,2,0,3:T(8,128)(2,1)S(1)} %copy.208), channel_id=1, replica_groups=mesh['item'=4,'var'=8] {'var'}, dimensions={3} | all-to-all | bytes 3145728 | tf_op jit(solution)/shard_map/all_to_all | solution.py:54
  86.3 2.8 copy.209
  89.0 3.7 reshape_reshape.20
  92.8 14.4 %multiply_reduce_fusion = (f32[2,2048]{1,0:T(2,128)S(1)}, f32[2,2048,2048]{1,2,0:T(8,128)}) fusion(bf16[1,2048,3,2,64]{1,4,3,2,0:T(8,128)(2,1)} %reshape_reshape.20), kind=kOutput, calls=%fused_computation.6 | convolution fusion | flops 1090514944 | bytes 34619392 | tf_op jit(solution)/shard_map/gshe,gkhe->ghsk/dot_general | solution.py:18
  107.2 13.6 %fusion = f32[2,2048]{1,0:T(2,128)S(1)} fusion(f32[2,2048,2048]{1,2,0:T(8,128)} %get-tuple-element.170, f32[2,2048]{1,0:T(2,128)S(1)} %get-tuple-element.169), kind=kLoop, calls=%fused_computation.4 | loop fusion | flops 25161728 | bytes 33587200 | tf_op jit(solution)/shard_map/reduce_sum | solution.py:70
  120.8 14.2 %fusion.90 = (bf16[1,2048,2,64]{1,3,2,0:T(8,128)(2,1)}, f32[1,2048,2,64]{1,3,2,0:T(8,128)}) fusion(f32[2,2048,2048]{1,2,0:T(8,128)} %get-tuple-element.170, f32[2,2048]{1,0:T(2,128)S(1)} %fusion, f32[2,2048]{1,0:T(2,128)S(1)} %get-tuple-element.169, bf16[1,2048,3,2,64]{1,4,3,2,0:T(8,128)(2,1)S(1)} %copy-done.5), kind=kOutput, calls=%fused_computation.181 | convolution fusion | flops 1107558400 | bytes 35684352 | tf_op jit(solution)/shard_map/ghsk,gkhe->gshe/dot_general | solution.py:18
  135.1 3.6 copy.211
  139.2 13.4 %reduce.16 = bf16[2048,128]{1,0:T(8,128)(2,1)} reduce(bf16[2048,1,1,1,128]{4,3,2,1,0:T(2,128)(2,1)} %bitcast.276, bf16[]{:T(256)} %broadcast.643), dimensions={1,2,3}, to_apply=%bitcast.204.reduce_sub_computation | reduce | bytes 1048578
  154.5 4.4 all-to-all-start.2
  160.9 7.7 %all-to-all-done.2 = bf16[8,2,16384]{2,1,0:T(2,128)(2,1)} async-done(((bf16[8,2,16384]{2,1,0:T(2,128)(2,1)}), bf16[8,2,16384]{2,1,0:T(2,128)(2,1)}, u32[]{:S(2)}, u32[]{:S(2)}) %all-to-all-start.2) | async-done | bytes 524320 | tf_op jit(solution)/shard_map/all_to_all | solution.py:60
  168.6 3.5 reshape.526
  178.6 6.5 multiply_convert_fusion.1
  185.1 4.3 convert_reduce_fusion
  189.4 2.7 multiply_reduce_fusion.5
  197.2 3.5 all-to-all-start.3
  200.8 3.4 convolution_convert_fusion.4
  204.3 6.1 all-to-all-done.3
  218.6 14.3 %multiply_convert_fusion = bf16[2,2048,2048]{1,2,0:T(8,128)(2,1)S(1)} fusion(f32[2,2048,2048]{1,2,0:T(8,128)} %get-tuple-element.170, f32[2,2048]{1,0:T(2,128)S(1)} %bitcast.294, f32[2,2048]{1,0:T(2,128)S(1)} %log_add_fusion, bf16[2048,2,64]{0,2,1:T(8,128)(2,1)S(1)} %reshape.496, bf16[1,2048,3,2,64]{1,4,3,2,0:T(8,128)(2,1)S(1)} %copy-done.6), kind=kOutput, calls=%fused_computation | convolution fusion | flops 1115684864 | bytes 51412992 | tf_op jit(solution)/shard_map/gshe,gkhe->ghsk/dot_general | solution.py:18
  232.9 5.7 copy-done.2
  238.6 3.9 fusion.19
  242.5 11.9 %fusion.20 = bf16[2,64,2048]{2,1,0:T(8,128)(2,1)} fusion(bf16[2,2048,2048]{1,2,0:T(8,128)(2,1)} %copy-done.2, bf16[1,2048,3,2,64]{1,4,3,2,0:T(8,128)(2,1)S(1)} %copy-done.6), kind=kOutput, calls=%fused_computation.40 | convolution fusion | flops 1074266112 | bytes 17825792 | tf_op jit(solution)/shard_map/ghsk,gshe->gkhe/dot_general | solution.py:18
  254.3 13.7 %fusion.16 = bf16[2,64,2048]{2,1,0:T(8,128)(2,1)S(1)} fusion(bf16[2048,2,64]{0,2,1:T(8,128)(2,1)S(1)} %reshape.496, f32[2,2048,2048]{1,2,0:T(8,128)} %get-tuple-element.170, f32[2,2048]{1,0:T(2,128)S(1)} %log_add_fusion), kind=kOutput, calls=%fused_computation.38 | convolution fusion | flops 1099169792 | bytes 34619392 | tf_op jit(solution)/shard_map/ghsk,gshe->gkhe/dot_general | solution.py:18
  272.7 5.0 maximum_bitcast_fusion
  277.8 29.0 %all_to_all.94 = bf16[1,2048,3,1,128]{4,2,3,0,1:T(4,128)(2,1)S(1)} all-to-all(bf16[1,2048,3,1,128]{4,2,3,0,1:T(4,128)(2,1)S(1)} %maximum_bitcast_fusion), channel_id=1, replica_groups=mesh['item'=4,'var'=8] {'var'}, dimensions={1} | all-to-all | bytes 3145728 | tf_op jit(solution)/shard_map/all_to_all | solution.py:60
  308.2 2.6 copy.224
  310.8 5.5 multiply_reduce_fusion.4
  318.9 4.6 convolution_convert_fusion.2
  324.7 7.6 %convolution_convert_fusion.1 = bf16[4096,1024]{1,0:T(8,128)(2,1)} fusion(bf16[256,4096]{1,0:T(8,128)(2,1)} %copy-done.16, f32[256,1024]{1,0:T(8,128)S(1)} %copy-done.10, f32[1024]{0:T(1024)S(1)} %convert_element_type.237, f32[1024]{0:T(1024)S(1)} %convert_element_type.236, f32[256]{0:T(256)S(1)} %add_rsqrt_fusion, f32[256]{0:T(256)S(1)} %broadcast_multiply_fusion.5), kind=kOutput, calls=%fused_computation.10 | convolution fusion | flops 2152988672 | bytes 11544576 | tf_op jit(solution)/shard_map/rf,rd->fd/dot_general | solution.py:18
  333.3 7.2 convolution_convert_fusion
  345.6 7.4 %fusion.35 = bf16[1,256,1024]{2,1,0:T(8,128)(2,1)} fusion(f32[256,1024]{1,0:T(8,128)S(1)} %copy-done.10, bf16[256,4096]{1,0:T(8,128)(2,1)} %get-tuple-element.175, bf16[4096,1024]{1,0:T(8,128)(2,1)} %param.39, f32[1024]{0:T(1024)S(1)} %convert_element_type.241), kind=kOutput, calls=%fused_computation.57 | convolution fusion | flops 2148270080 | bytes 12062720 | tf_op jit(solution)/shard_map/dot_general | solution.py:180
  363.9 60.8 %reduce-scatter.8.cloned.1.call-done = bf16[384,1024]{1,0:T(8,128)(2,1)} async-done(((bf16[3072,1024]{1,0:T(8,128)(2,1)}), bf16[384,1024]{1,0:T(8,128)(2,1)}) %reduce-scatter.8.cloned.1.call-update) | async-done | bytes 786448 | tf_op jit(solution)/shard_map/reduce_scatter | solution.py:272
  424.7 74.8 %reduce-scatter.12.cloned.1.call-done = bf16[512,1024]{1,0:T(8,128)(2,1)} async-done(((bf16[4096,1024]{1,0:T(8,128)(2,1)}), bf16[512,1024]{1,0:T(8,128)(2,1)}) %reduce-scatter.12.cloned.1.call-update) | async-done | bytes 1048592 | tf_op jit(solution)/shard_map/reduce_scatter | solution.py:272
  499.5 74.8 %reduce-scatter.14.cloned.1.call-done = bf16[128,4096]{1,0:T(8,128)(2,1)} async-done(((bf16[1024,4096]{1,0:T(8,128)(2,1)}), bf16[128,4096]{1,0:T(8,128)(2,1)}) %reduce-scatter.14.cloned.1.call-update) | async-done | bytes 1048592 | tf_op jit(solution)/shard_map/reduce_scatter | solution.py:272
  574.5 2.6 subtract_multiply_fusion.2
  577.9 58.4 %all-reduce.10 = (f32[13056]{0:T(1024)S(1)}, bf16[240,1024]{1,0:T(8,128)(2,1)S(1)}) all-reduce(f32[13056]{0:T(1024)S(1)} %constant_dynamic-update-slice_fusion, f32[240,1024]{1,0:T(8,128)S(1)} %reshape.504), channel_id=1, replica_groups=mesh['item'=4,'var'=8] {'item','var'}, use_global_device_ids=true, to_apply=%region_27.28 | all-reduce | flops 258816 | bytes 1579008 | tf_op jit(solution)/shard_map/psum | solution.py:237
  651.4 3.4 all-to-all-start.5
  656.5 2.9 broadcast_multiply_fusion
  662.7 47.9 %all-reduce.9.cloned.1.call-done = (bf16[1024,128]{0,1:T(8,128)(2,1)}, bf16[1024,384]{0,1:T(8,128)(2,1)}, bf16[1024,128]{0,1:T(8,128)(2,1)}, bf16[1024,512]{0,1:T(8,128)(2,1)}, bf16[4096,128]{0,1:T(8,128)(2,1)}) async-done(((bf16[1024,128]{0,1:T(8,128)(2,1)}, bf16[1024,384]{0,1:T(8,128)(2,1)}, bf16[1024,128]{0,1:T(8,128)(2,1)}, bf16[1024,512]{0,1:T(8,128)(2,1)}, bf16[4096,128]{0,1:T(8,128)(2,1)}), ...) | async-done | bytes 3407888 | tf_op jit(solution)/shard_map/psum | solution.py:273
  710.6 2.7 copy.239
  (332 shorter events, 87.7 us)
Async XLA Ops:
  7.2 169.0 %copy-start = (bf16[1024,1024]{1,0:T(8,128)(2,1)S(1)}, bf16[1024,1024]{1,0:T(8,128)(2,1)}, u32[]{:S(2)}) copy-start(bf16[1024,1024]{1,0:T(8,128)(2,1)} %param.34) | copy-start | bytes 6291460
  7.2 17.3 %copy-start.85 = (bf16[1024]{0:T(1024)(128)(2,1)S(1)}, bf16[1024]{0:T(1024)(128)(2,1)}, u32[]{:S(2)}) copy-start(bf16[1024]{0:T(1024)(128)(2,1)} %param.27) | copy-start | bytes 6148
  7.2 17.3 %copy-start.62 = (bf16[8,4,1024]{2,1,0:T(4,128)(2,1)S(1)}, bf16[8,4,1024]{2,1,0:T(4,128)(2,1)}, u32[]{:S(2)}) copy-start(bf16[8,4,1024]{2,1,0:T(4,128)(2,1)} %param.25) | copy-start | bytes 196612
  7.2 17.3 %copy-start.70 = (bf16[8,1024]{1,0:T(8,128)(2,1)S(1)}, bf16[8,1024]{1,0:T(8,128)(2,1)}, u32[]{:S(2)}) copy-start(bf16[8,1024]{1,0:T(8,128)(2,1)} %param.26) | copy-start | bytes 49156
  15.3 28.7 %all-to-all-start = ((bf16[8,2,4096]{2,1,0:T(2,128)(2,1)}), bf16[8,2,4096]{2,1,0:T(2,128)(2,1)S(1)}, u32[]{:S(2)}, u32[]{:S(2)}) async-start(bf16[8,2,4096]{2,1,0:T(2,128)(2,1)} %reshape.523), calls=%async_computation | async-start | bytes 262144 | tf_op jit(solution)/shard_map/all_to_all | solution.py:126
  20.5 19.1 %copy-start.76 = (s32[5,64]{1,0:T(8,128)S(1)}, s32[5,64]{1,0:T(8,128)}, u32[]{:S(2)}) copy-start(s32[5,64]{1,0:T(8,128)} %param.23) | copy-start | bytes 3844
  38.9 14.3 %copy-start.50 = (f32[16,48]{1,0:T(8,128)}, f32[16,48]{1,0:T(8,128)S(1)}, u32[]{:S(2)}) copy-start(f32[16,48]{1,0:T(8,128)S(1)} %get-tuple-element.162) | copy-start | bytes 9220
  38.9 14.3 %copy-start.52 = (f32[16,48]{1,0:T(8,128)}, f32[16,48]{1,0:T(8,128)S(1)}, u32[]{:S(2)}) copy-start(f32[16,48]{1,0:T(8,128)S(1)} %get-tuple-element.163) | copy-start | bytes 9220
  38.9 14.3 %copy-start.54 = (f32[16,48]{1,0:T(8,128)}, f32[16,48]{1,0:T(8,128)S(1)}, u32[]{:S(2)}) copy-start(f32[16,48]{1,0:T(8,128)S(1)} %get-tuple-element.164) | copy-start | bytes 9220
  38.9 14.3 %copy-start.56 = (f32[16,48]{1,0:T(8,128)}, f32[16,48]{1,0:T(8,128)S(1)}, u32[]{:S(2)}) copy-start(f32[16,48]{1,0:T(8,128)S(1)} %get-tuple-element.165) | copy-start | bytes 9220
  38.9 14.3 %copy-start.58 = (f32[16,48]{1,0:T(8,128)}, f32[16,48]{1,0:T(8,128)S(1)}, u32[]{:S(2)}) copy-start(f32[16,48]{1,0:T(8,128)S(1)} %get-tuple-element.166) | copy-start | bytes 9220
  40.1 13.2 %copy-start.79 = (f32[48]{0:T(128)}, f32[48]{0:T(128)S(1)}, u32[]{:S(2)}) copy-start(f32[48]{0:T(128)S(1)} %broadcast_in_dim_reshape.3) | copy-start | bytes 580
  43.9 12.7 %copy-start.64 = (f32[1024]{0:T(1024)}, f32[1024]{0:T(1024)S(1)}, u32[]{:S(2)}) copy-start(f32[1024]{0:T(1024)S(1)} %convert_element_type.230) | copy-start | bytes 12292
  43.9 12.7 %copy-start.68 = (f32[1024]{0:T(1024)}, f32[1024]{0:T(1024)S(1)}, u32[]{:S(2)}) copy-start(f32[1024]{0:T(1024)S(1)} %convert_element_type.231) | copy-start | bytes 12292
  107.2 13.7 %copy-start.5 = (bf16[1,2048,3,2,64]{1,4,3,2,0:T(8,128)(2,1)S(1)}, bf16[1,2048,3,2,64]{1,4,3,2,0:T(8,128)(2,1)}, u32[]{:S(2)}) copy-start(bf16[1,2048,3,2,64]{1,4,3,2,0:T(8,128)(2,1)} %reshape_reshape.20) | copy-start | bytes 4718596
  135.1 23.8 %copy-start.83 = (bf16[1024]{0:T(1024)(128)(2,1)S(1)}, bf16[1024]{0:T(1024)(128)(2,1)}, u32[]{:S(2)}) copy-start(bf16[1024]{0:T(1024)(128)(2,1)} %param.35) | copy-start | bytes 6148
  135.1 23.8 %copy-start.84 = (bf16[1024]{0:T(1024)(128)(2,1)S(1)}, bf16[1024]{0:T(1024)(128)(2,1)}, u32[]{:S(2)}) copy-start(bf16[1024]{0:T(1024)(128)(2,1)} %param.36) | copy-start | bytes 6148
  135.1 23.9 %copy-start.75 = (bf16[4096]{0:T(1024)(128)(2,1)S(1)}, bf16[4096]{0:T(1024)(128)(2,1)}, u32[]{:S(2)}) copy-start(bf16[4096]{0:T(1024)(128)(2,1)} %param.38) | copy-start | bytes 24580
  135.1 23.9 %copy-start.87 = (s32[5]{0:T(128)S(1)}, s32[5]{0:T(128)}, u32[]{:S(2)}) copy-start(s32[5]{0:T(128)} %param.24) | copy-start | bytes 64
  154.5 14.1 %all-to-all-start.2 = ((bf16[8,2,16384]{2,1,0:T(2,128)(2,1)}), bf16[8,2,16384]{2,1,0:T(2,128)(2,1)}, u32[]{:S(2)}, u32[]{:S(2)}) async-start(bf16[8,2,16384]{2,1,0:T(2,128)(2,1)} %reshape.525), calls=%async_computation.2 | async-start | bytes 1048576 | tf_op jit(solution)/shard_map/all_to_all | solution.py:60
  178.2 13.9 %copy-start.9 = (f32[256,1024]{1,0:T(8,128)}, f32[256,1024]{1,0:T(8,128)S(1)}, u32[]{:S(2)}) copy-start(f32[256,1024]{1,0:T(8,128)S(1)} %get-tuple-element.174) | copy-start | bytes 3145732
  197.2 13.2 %all-to-all-start.3 = ((bf16[1,256,1,8,128]{1,4,2,0,3:T(8,128)(2,1)}), bf16[1,256,1,8,128]{1,4,2,0,3:T(8,128)(2,1)S(1)}, u32[]{:S(2)}, u32[]{:S(2)}) async-start(bf16[1,256,1,8,128]{1,4,2,0,3:T(8,128)(2,1)} %bitcast.38), calls=%async_computation.3 | async-start | bytes 1048576 | tf_op jit(solution)/shard_map/all_to_all | solution.py:54
  200.7 163.2 %reduce-scatter.10.cloned.1.call-start = ((), (), s32[]{:S(2)}) async-start(), calls=%async_computation.13 | async-start | bytes 2359296 | tf_op jit(solution)/shard_map/reduce_scatter | solution.py:272
  204.2 159.7 %reduce-scatter.6.cloned.1.call-start = ((), (), s32[]{:S(2)}) async-start(), calls=%async_computation.11 | async-start | bytes 2359296 | tf_op jit(solution)/shard_map/reduce_scatter | solution.py:272
  254.3 13.7 %copy-start.15 = (bf16[2,64,2048]{2,1,0:T(8,128)(2,1)S(1)}, bf16[2,64,2048]{2,1,0:T(8,128)(2,1)}, u32[]{:S(2)}) copy-start(bf16[2,64,2048]{2,1,0:T(8,128)(2,1)} %fusion.19) | copy-start | bytes 1572868
  254.3 15.7 %copy-start.14 = (bf16[2,64,2048]{2,1,0:T(8,128)(2,1)S(1)}, bf16[2,64,2048]{2,1,0:T(8,128)(2,1)}, u32[]{:S(2)}) copy-start(bf16[2,64,2048]{2,1,0:T(8,128)(2,1)} %fusion.20) | copy-start | bytes 1572868
  318.9 105.8 %reduce-scatter.8.cloned.1.call-start = ((), (), s32[]{:S(2)}) async-start(), calls=%async_computation.12 | async-start | bytes 7077888 | tf_op jit(solution)/shard_map/reduce_scatter | solution.py:272
  323.5 176.0 %reduce-scatter.12.cloned.1.call-start = ((), (), s32[]{:S(2)}) async-start(), calls=%async_computation.14 | async-start | bytes 9437184 | tf_op jit(solution)/shard_map/reduce_scatter | solution.py:272
  332.3 242.0 %reduce-scatter.14.cloned.1.call-start = ((), (), s32[]{:S(2)}) async-start(), calls=%async_computation.15 | async-start | bytes 9437184 | tf_op jit(solution)/shard_map/reduce_scatter | solution.py:272
  340.6 370.0 %all-reduce.9.cloned.1.call-start = ((), (), s32[]{:S(2)}) async-start(), calls=%async_computation.16 | async-start | bytes 6815744 | tf_op jit(solution)/shard_map/psum | solution.py:273
  362.4 212.0 %copy-start.36 = (f32[1,1,48,256]{3,2,1,0:T(8,128)S(1)}, f32[1,1,48,256]{3,2,1,0:T(8,128)}, u32[]{:S(2)}) copy-start(f32[1,1,48,256]{3,2,1,0:T(8,128)} %copy-done.35) | copy-start | bytes 147460
  362.4 212.0 %copy-start.38 = (f32[48,256]{1,0:T(8,128)S(1)}, f32[48,256]{1,0:T(8,128)}, u32[]{:S(2)}) copy-start(f32[48,256]{1,0:T(8,128)} %copy-done.37) | copy-start | bytes 147460
  362.4 212.0 %copy-start.40 = (f32[48,256]{1,0:T(8,128)S(1)}, f32[48,256]{1,0:T(8,128)}, u32[]{:S(2)}) copy-start(f32[48,256]{1,0:T(8,128)} %copy-done.39) | copy-start | bytes 147460
  362.4 212.0 %copy-start.42 = (f32[48,256]{1,0:T(8,128)S(1)}, f32[48,256]{1,0:T(8,128)}, u32[]{:S(2)}) copy-start(f32[48,256]{1,0:T(8,128)} %copy-done.41) | copy-start | bytes 147460
  362.4 212.0 %copy-start.44 = (f32[48,256]{1,0:T(8,128)S(1)}, f32[48,256]{1,0:T(8,128)}, u32[]{:S(2)}) copy-start(f32[48,256]{1,0:T(8,128)} %copy-done.43) | copy-start | bytes 147460
  362.4 212.0 %copy-start.51 = (f32[16,48]{1,0:T(8,128)S(1)}, f32[16,48]{1,0:T(8,128)}, u32[]{:S(2)}) copy-start(f32[16,48]{1,0:T(8,128)} %copy-done.50) | copy-start | bytes 9220
  362.4 212.0 %copy-start.53 = (f32[16,48]{1,0:T(8,128)S(1)}, f32[16,48]{1,0:T(8,128)}, u32[]{:S(2)}) copy-start(f32[16,48]{1,0:T(8,128)} %copy-done.52) | copy-start | bytes 9220
  362.4 212.0 %copy-start.55 = (f32[16,48]{1,0:T(8,128)S(1)}, f32[16,48]{1,0:T(8,128)}, u32[]{:S(2)}) copy-start(f32[16,48]{1,0:T(8,128)} %copy-done.54) | copy-start | bytes 9220
  362.5 212.0 %copy-start.57 = (f32[16,48]{1,0:T(8,128)S(1)}, f32[16,48]{1,0:T(8,128)}, u32[]{:S(2)}) copy-start(f32[16,48]{1,0:T(8,128)} %copy-done.56) | copy-start | bytes 9220
  362.5 212.0 %copy-start.59 = (f32[16,48]{1,0:T(8,128)S(1)}, f32[16,48]{1,0:T(8,128)}, u32[]{:S(2)}) copy-start(f32[16,48]{1,0:T(8,128)} %copy-done.58) | copy-start | bytes 9220
  362.5 212.0 %copy-start.61 = (f32[16,256]{1,0:T(8,128)S(1)}, f32[16,256]{1,0:T(8,128)}, u32[]{:S(2)}) copy-start(f32[16,256]{1,0:T(8,128)} %copy-done.60) | copy-start | bytes 49156
  362.5 212.0 %copy-start.67 = (f32[16,256]{1,0:T(8,128)S(1)}, f32[16,256]{1,0:T(8,128)}, u32[]{:S(2)}) copy-start(f32[16,256]{1,0:T(8,128)} %copy-done.66) | copy-start | bytes 49156
  362.5 212.0 %copy-start.78 = (pred[48]{0:T(512)(128)(4,1)S(1)}, pred[48]{0:T(512)(128)(4,1)}, u32[]{:S(2)}) copy-start(pred[48]{0:T(512)(128)(4,1)} %copy-done.77) | copy-start | bytes 148
  362.5 212.0 %copy-start.80 = (f32[48]{0:T(128)S(1)}, f32[48]{0:T(128)}, u32[]{:S(2)}) copy-start(f32[48]{0:T(128)} %copy-done.79) | copy-start | bytes 580
  577.1 64.6 %copy-start.47 = (bf16[1024,16]{0,1:T(8,128)(2,1)S(1)}, bf16[1024,16]{0,1:T(8,128)(2,1)}, u32[]{:S(2)}) copy-start(bf16[1024,16]{0,1:T(8,128)(2,1)} %copy-done.46) | copy-start | bytes 98308
  641.9 14.2 %copy-start.13 = (bf16[48,5,1024]{2,0,1:T(8,128)(2,1)S(1)}, bf16[48,5,1024]{2,0,1:T(8,128)(2,1)}, u32[]{:S(2)}) copy-start(bf16[48,5,1024]{2,0,1:T(8,128)(2,1)} %copy-done.12) | copy-start | bytes 1474564
  644.5 12.0 %copy-start.88 = (f32[128]{0:T(128)S(1)}, f32[128]{0:T(128)}, u32[]{:S(2)}) copy-start(f32[128]{0:T(128)} %dynamic_slice.40) | copy-start | bytes 1540
  651.4 10.5 %all-to-all-start.5 = ((bf16[1,64,4,256]{3,2,0,1:T(4,128)(2,1)}), bf16[1,64,4,256]{3,2,0,1:T(4,128)(2,1)S(1)}, u32[]{:S(2)}, u32[]{:S(2)}) async-start(bf16[1,64,4,256]{3,2,0,1:T(4,128)(2,1)} %bitcast.72), calls=%async_computation.5 | async-start | bytes 262144 | tf_op jit(solution)/shard_map/all_to_all | solution.py:223
  (57 other events, 276.0 us)
Sparse Core Ops, SparseCore 0:
  204.8 42.7 reduce-scatter.9
  319.0 40.4 reduce-scatter.5
  362.9 61.7 reduce-scatter.7
  428.0 71.4 reduce-scatter.11
  502.8 71.4 reduce-scatter.13
  577.0 133.6 all-reduce.8

commit v2 on v1

--- a/solution.py
+++ b/solution.py
@@ -1,6 +1,10 @@
+import functools
+
 import jax
 import jax.numpy as jnp
 from jax import lax
+from jax.experimental import pallas as pl
+from jax.experimental.pallas import tpu as pltpu
 from jax.sharding import PartitionSpec as P
 
 D = 1024
@@ -12,6 +16,8 @@
 FACTOR = HEAD_DIM ** (-0.5)
 F32 = jnp.float32
 BF16 = jnp.bfloat16
+MESH = pl.DeviceIdType.MESH
+KEY_PARTS = 4
 
 
 def mm(spec, a, b):
@@ -46,21 +52,6 @@
     pads[axis + 1] = (0, 1)
     full = jnp.pad(array.reshape(split), pads)
     return full.reshape(shape[:axis] + (shape[axis] // 3 * 4,) + shape[axis + 1 :])
-
-
-def to_heads(rows, lanes, parts):
-    g, r, _ = rows.shape
-    wide = rows.reshape(g, r, parts, lanes, D // lanes)
-    out = lax.all_to_all(wide, "var", split_axis=3, concat_axis=1, tiled=True)
-    return out.reshape(g, r * lanes, parts, D // lanes)
-
-
-def from_heads(cols, lanes):
-    g, p, parts, w = cols.shape
-    out = lax.all_to_all(
-        cols.reshape(g, p, parts, 1, w), "var", split_axis=1, concat_axis=3, tiled=True
-    )
-    return out.reshape(g, p // lanes, parts * w * lanes)
 
 
 def attention_forward(queries, keys, values):
@@ -80,6 +71,310 @@
     g_k = mm("ghsk,gshe->gkhe", g_scores, queries) * FACTOR
     g_v = mm("ghsk,gshe->gkhe", probs.astype(BF16), g_att)
     return g_q, g_k, g_v
+
+
+def greet(me, n):
+    barrier = pltpu.get_barrier_semaphore()
+    for i in range(1, n):
+        pl.semaphore_signal(
+            barrier, inc=1, device_id={"var": lax.rem(me + i, n)}, device_id_type=MESH
+        )
+    pl.semaphore_wait(barrier, n - 1)
+
+
+def nt(a, b):
+    return lax.dot_general(a, b, (((1,), (1,)), ((), ())), preferred_element_type=F32)
+
+
+def nn(a, b):
+    return jnp.dot(a, b, preferred_element_type=F32)
+
+
+def head_masks(width):
+    lane = lax.broadcasted_iota(jnp.int32, (1, width), 1) // HEAD_DIM
+    return [(lane == h).astype(F32) for h in range(width // HEAD_DIM)]
+
+
+def forward_kernel(
+    n, qkv, heads, o_out, lse_out, att_out, recv, land, obuf, v_t, s_buf,
+    send, got, back_send, back_got, out_sem,
+):
+    me = lax.axis_index("var")
+    rows, total = qkv.shape
+    dim = total // 3
+    width = dim // n
+    patches = rows * n
+    mine = pl.ds(pl.multiple_of(me * rows, rows), rows)
+    own_lanes = pl.ds(pl.multiple_of(me * width, width), width)
+    greet(me, n)
+
+    def out_copy(s, i):
+        to = lax.rem(me + i, n)
+        return pltpu.make_async_remote_copy(
+            src_ref=qkv.at[:, pl.ds(pl.multiple_of(s * dim + to * width, width), width)],
+            dst_ref=recv.at[s, mine, :],
+            send_sem=send.at[s, i],
+            recv_sem=got.at[s, i],
+            device_id={"var": to},
+            device_id_type=MESH,
+        )
+
+    def back_copy(i):
+        to = lax.rem(me - i + n, n)
+        return pltpu.make_async_remote_copy(
+            src_ref=obuf.at[i],
+            dst_ref=land.at[:, own_lanes],
+            send_sem=back_send.at[i],
+            recv_sem=back_got.at[i],
+            device_id={"var": to},
+            device_id_type=MESH,
+        )
+
+    for s in (1, 2, 0):
+        for i in range(1, n):
+            out_copy(s, i).start()
+    for s in (1, 2, 0):
+        recv[s, mine, :] = qkv[:, pl.ds(pl.multiple_of(s * dim + me * width, width), width)]
+    masks = head_masks(width)
+    for s in (1, 2):
+        for i in range(1, n):
+            out_copy(s, i).wait_recv()
+    v_t[...] = recv[2].T
+    chunk = s_buf.shape[0] // KEY_PARTS
+
+    def block(i, carry):
+        source = lax.rem(me - i + n, n)
+
+        @pl.when(i > 0)
+        def _():
+            out_copy(0, i).wait_recv()
+
+        place = pl.ds(pl.multiple_of(source * rows, rows), rows)
+        q = recv[0, place, :].astype(F32) * FACTOR
+        outs = []
+        for h, mask in enumerate(masks):
+            qh = (q * mask).astype(BF16)
+            high = None
+            for c in range(KEY_PARTS):
+                part = slice(c * chunk, (c + 1) * chunk)
+                scores = nt(recv[1, part, :], qh)
+                s_buf[part, :] = scores
+                top = jnp.max(scores, axis=0, keepdims=True)
+                high = top if high is None else jnp.maximum(high, top)
+            sums = jnp.zeros_like(high)
+            acc = jnp.zeros((HEAD_DIM, rows), F32)
+            for c in range(KEY_PARTS):
+                part = slice(c * chunk, (c + 1) * chunk)
+                terms = jnp.exp(s_buf[part, :] - high)
+                sums = sums + jnp.sum(terms, axis=0, keepdims=True)
+                acc = acc + nn(v_t[h * HEAD_DIM : (h + 1) * HEAD_DIM, part], terms.astype(BF16))
+            lse_out[h : h + 1, place] = high + jnp.log(sums)
+            outs.append(acc / sums)
+        o_t = jnp.concatenate(outs, axis=0)
+        o_out[:, place] = o_t
+        obuf[i] = o_t.T.astype(BF16)
+
+        @pl.when(i > 0)
+        def _():
+            back_copy(i).start()
+
+        return carry
+
+    lax.fori_loop(0, n, block, 0)
+    save = pltpu.make_async_copy(recv, heads, out_sem)
+    save.start()
+    land[:, own_lanes] = obuf[0]
+    for i in range(1, n):
+        for s in range(3):
+            out_copy(s, i).wait_send()
+        back_copy(i).wait_send()
+        back_copy(i).wait_recv()
+    att_out[...] = land[...]
+    save.wait()
+
+
+def backward_kernel(
+    n, g_in, heads, o_t, lse, gh_out, gq_out, g_all, land, dk, dv, k_t,
+    send, got, q_send, q_got, kv_send, kv_got,
+):
+    me = lax.axis_index("var")
+    rows, dim = g_in.shape
+    width = dim // n
+    patches = rows * n
+    mine = pl.ds(pl.multiple_of(me * rows, rows), rows)
+    own_lanes = pl.ds(pl.multiple_of(me * width, width), width)
+    greet(me, n)
+
+    def out_copy(i):
+        to = lax.rem(me + i, n)
+        return pltpu.make_async_remote_copy(
+            src_ref=g_in.at[:, pl.ds(pl.multiple_of(to * width, width), width)],
+            dst_ref=g_all.at[mine, :],
+            send_sem=send.at[i],
+            recv_sem=got.at[i],
+            device_id={"var": to},
+            device_id_type=MESH,
+        )
+
+    def part_lanes(s):
+        return pl.ds(pl.multiple_of(s * dim + me * width, width), width)
+
+    def q_copy(i):
+        to = lax.rem(me - i + n, n)
+        return pltpu.make_async_remote_copy(
+            src_ref=gh_out.at[0, pl.ds(pl.multiple_of(to * rows, rows), rows), :],
+            dst_ref=land.at[:, part_lanes(0)],
+            send_sem=q_send.at[i],
+            recv_sem=q_got.at[i],
+            device_id={"var": to},
+            device_id_type=MESH,
+        )
+
+    def kv_copy(s, i):
+        to = lax.rem(me + i, n)
+        return pltpu.make_async_remote_copy(
+            src_ref=gh_out.at[s, pl.ds(pl.multiple_of(to * rows, rows), rows), :],
+            dst_ref=land.at[:, part_lanes(s)],
+            send_sem=kv_send.at[s - 1, i],
+            recv_sem=kv_got.at[s - 1, i],
+            device_id={"var": to},
+            device_id_type=MESH,
+        )
+
+    for i in range(1, n):
+        out_copy(i).start()
+    g_all[mine, :] = g_in[:, own_lanes]
+    masks = head_masks(width)
+    k_t[...] = heads[1].T
+    dk[...] = jnp.zeros_like(dk)
+    dv[...] = jnp.zeros_like(dv)
+    chunk = patches // KEY_PARTS
+
+    def block(i, carry):
+        source = lax.rem(me - i + n, n)
+
+        @pl.when(i > 0)
+        def _():
+            out_copy(i).wait_recv()
+
+        place = pl.ds(pl.multiple_of(source * rows, rows), rows)
+        q = heads[0, place, :].astype(F32) * FACTOR
+        grad = g_all[place, :].astype(F32)
+        products = grad.T * o_t[:, place]
+        outs = []
+        for h, mask in enumerate(masks):
+            qh = (q * mask).astype(BF16)
+            gh = (grad * mask).astype(BF16)
+            span = slice(h * HEAD_DIM, (h + 1) * HEAD_DIM)
+            rowdot = jnp.sum(products[span], axis=0, keepdims=True)
+            total = lse[h : h + 1, place]
+            acc = jnp.zeros((HEAD_DIM, rows), F32)
+            for c in range(KEY_PARTS):
+                part = slice(c * chunk, (c + 1) * chunk)
+                probs = jnp.exp(nt(heads[1, part, :], qh) - total)
+                g_probs = nt(heads[2, part, :], gh)
+                g_scores = (probs * (g_probs - rowdot)).astype(BF16)
+                dv[part, :] += nn(probs.astype(BF16), gh)
+                dk[part, :] += nn(g_scores, qh)
+                acc = acc + nn(k_t[span, part], g_scores)
+            outs.append(acc * FACTOR)
+        gh_out[0, place, :] = jnp.concatenate(outs, axis=0).T.astype(BF16)
+
+        @pl.when(i > 0)
+        def _():
+            q_copy(i).start()
+
+        return carry
+
+    lax.fori_loop(0, n, block, 0)
+    gh_out[1] = dk[...].astype(BF16)
+    gh_out[2] = dv[...].astype(BF16)
+    for i in range(1, n):
+        for s in (1, 2):
+            kv_copy(s, i).start()
+    for s in range(3):
+        land[:, part_lanes(s)] = gh_out[s, mine, :]
+    for i in range(1, n):
+        out_copy(i).wait_send()
+        q_copy(i).wait_send()
+        q_copy(i).wait_recv()
+        for s in (1, 2):
+            kv_copy(s, i).wait_send()
+            kv_copy(s, i).wait_recv()
+    gq_out[...] = land[...]
+
+
+VMEM = pl.BlockSpec(memory_space=pltpu.VMEM)
+
+
+def attention_forward_call(qkv, n):
+    rows, total = qkv.shape
+    dim = total // 3
+    width = dim // n
+    patches = rows * n
+    sems = pltpu.SemaphoreType.DMA
+    return pl.pallas_call(
+        functools.partial(forward_kernel, n),
+        out_shape=(
+            jax.ShapeDtypeStruct((3, patches, width), BF16),
+            jax.ShapeDtypeStruct((width, patches), F32),
+            jax.ShapeDtypeStruct((width // HEAD_DIM, patches), F32),
+            jax.ShapeDtypeStruct((rows, dim), BF16),
+        ),
+        in_specs=[VMEM],
+        out_specs=(pl.BlockSpec(memory_space=pl.ANY), VMEM, VMEM, VMEM),
+        scratch_shapes=[
+            pltpu.VMEM((3, patches, width), BF16),
+            pltpu.VMEM((rows, dim), BF16),
+            pltpu.VMEM((n, rows, width), BF16),
+            pltpu.VMEM((width, patches), BF16),
+            pltpu.VMEM((patches, rows), F32),
+            sems((3, n)),
+            sems((3, n)),
+            sems((n,)),
+            sems((n,)),
+            sems,
+        ],
+        compiler_params=pltpu.CompilerParams(collective_id=0, has_side_effects=True),
+        cost_estimate=pl.CostEstimate(
+            flops=40_000_000_000, bytes_accessed=8_000_000, transcendentals=0
+        ),
+        name="attention_forward",
+    )(qkv)
+
+
+def attention_backward_call(g_att, heads, o_t, lse, n):
+    rows, dim = g_att.shape
+    width = dim // n
+    patches = rows * n
+    sems = pltpu.SemaphoreType.DMA
+    return pl.pallas_call(
+        functools.partial(backward_kernel, n),
+        out_shape=(
+            jax.ShapeDtypeStruct((3, patches, width), BF16),
+            jax.ShapeDtypeStruct((rows, 3 * dim), BF16),
+        ),
+        in_specs=[VMEM] * 4,
+        out_specs=(VMEM, VMEM),
+        scratch_shapes=[
+            pltpu.VMEM((patches, width), BF16),
+            pltpu.VMEM((rows, 3 * dim), BF16),
+            pltpu.VMEM((patches, width), F32),
+            pltpu.VMEM((patches, width), F32),
+            pltpu.VMEM((width, patches), BF16),
+            sems((n,)),
+            sems((n,)),
+            sems((n,)),
+            sems((n,)),
+            sems((2, n)),
+            sems((2, n)),
+        ],
+        compiler_params=pltpu.CompilerParams(collective_id=1, has_side_effects=True),
+        cost_estimate=pl.CostEstimate(
+            flops=60_000_000_000, bytes_accessed=8_000_000, transcendentals=0
+        ),
+        name="attention_backward",
+    )(g_att, heads, o_t, lse)
 
 
 def body(
@@ -153,22 +448,16 @@
     first = (normed1 * gain1 + shift1).astype(BF16)
     qkv = jnp.dot(first, qkv_weight, preferred_element_type=F32).astype(BF16).reshape(g, r, 3 * D)
 
-    by_head = HEADS % lanes == 0
+    by_head = HEAD_DIM * HEADS == 128 * lanes and g == 1
     if by_head:
-        own_heads = HEADS // lanes
-        heads = to_heads(qkv, lanes, 3).reshape(g, PATCHES, 3, own_heads, HEAD_DIM)
-        queries, keys, values = heads[:, :, 0], heads[:, :, 1], heads[:, :, 2]
+        heads, o_t, lse, attended = attention_forward_call(qkv[0], lanes)
     else:
         queries = qkv[..., :D].reshape(g, r, HEADS, HEAD_DIM)
         pair = lax.all_gather(qkv[..., D:], "var", axis=1, tiled=True)
         pair = pair.reshape(g, PATCHES, 2, HEADS, HEAD_DIM)
         keys, values = pair[:, :, 0], pair[:, :, 1]
-    att_full, lse = attention_forward(queries, keys, values)
-    att = att_full.astype(BF16).reshape(g, att_full.shape[1], -1)
-    if by_head:
-        attended = from_heads(att[:, :, None, :], lanes).reshape(rows, D)
-    else:
-        attended = att.reshape(rows, D)
+        att_full, lse = attention_forward(queries, keys, values)
+        attended = att_full.astype(BF16).reshape(rows, D)
 
     residual = result + jnp.dot(attended, proj_weight, preferred_element_type=F32)
     normed2, inv2 = norm_stats(residual)
@@ -188,17 +477,14 @@
     g_resid = g_final + norm_back(g_second, gain2, normed2, inv2)
     g_branch = g_resid.astype(BF16)
     proj_t = mm("re,rd->ed", g_branch, attended).astype(BF16)
-    g_att = mm("re,de->rd", g_branch, proj_weight).astype(BF16).reshape(g, r, D)
+    g_att = mm("re,de->rd", g_branch, proj_weight).astype(BF16)
     if by_head:
-        g_att = to_heads(g_att, lanes, 1)
-    g_att = g_att.reshape(att_full.shape)
-    rowdot = jnp.transpose(jnp.sum(g_att.astype(F32) * att_full, axis=-1), (0, 2, 1))[..., None]
-    g_q, g_k, g_v = attention_back(queries, keys, values, g_att, lse, rowdot)
-    if by_head:
-        width = D // lanes
-        parts = [t.astype(BF16).reshape(g, PATCHES, 1, width) for t in (g_q, g_k, g_v)]
-        g_qkv = from_heads(jnp.concatenate(parts, axis=2), lanes)
+        g_heads, g_qkv = attention_backward_call(g_att, heads, o_t, lse, lanes)
     else:
+        g_att = g_att.reshape(att_full.shape)
+        rowdot = jnp.sum(g_att.astype(F32) * att_full, axis=-1)
+        rowdot = jnp.transpose(rowdot, (0, 2, 1))[..., None]
+        g_q, g_k, g_v = attention_back(queries, keys, values, g_att, lse, rowdot)
         parts = [
             lax.psum_scatter(t, "var", scatter_dimension=1, tiled=True).reshape(g, r, D)
             for t in (g_k, g_v)

time: 737 us -> 598 us (0.81)
  Pallas kernels: 0 us -> 83.3 us
  matrix products: 147 us -> 76.6 us
  blocking collectives: 122 us -> 70.5 us
  local copies, waits for them, and re-layouts: 101 us -> 54.4 us
  other arithmetic: 48.6 us -> 14.7 us
  starting transfers between devices: 16.9 us -> 9.2 us
    pallas_call x0 -> x2, Pallas kernels: none -> 83.3 us  [the longest x1 43.4 us: attention_backward_call(): pl.pallas_call(functools.partial(backward_kernel, n), out_shape=(jax.Shap...]
    dot_general x22 -> x16, matrix products: 120 us -> 49.6 us  [mm(): return jnp.einsum(spec, a, b, preferred_element_type=F32)]
    all_to_all x2 -> x0, blocking collectives: 53.3 us -> none  [the longest x1 29 us: from_heads(): lax.all_to_all(cols.reshape(g, p, parts, 1, w), 'var', split_axis=1, conc...]
    reduce_sum x2 -> x0, other arithmetic: 15.4 us -> none  [the longest x1 13.6 us: attention_forward(): totals = jnp.sum(terms, axis=-1, keepdims=True)]
    all_to_all x2 -> x0, waiting for transfers between devices: 13.8 us -> none  [the longest x1 7.71 us: from_heads(): lax.all_to_all(cols.reshape(g, p, parts, 1, w), 'var', split_axis=1, conc...]
    unnamed x215 -> x176, local copies, waits for them, and re-layouts: 46.7 us -> 33.3 us
    unnamed x5 -> x4, other arithmetic: 13.4 us -> 0.08 us
    another operation x6 -> x1, local copies, waits for them, and re-layouts: 11.1 us -> 0.08 us  [the longest x1 3.74 us: body(): heads = to_heads(qkv, lanes, 3).reshape(g, PATCHES, 3, own_heads, HEAD_DIM)]
  transfers between devices with their start and end apart: 10 -> 8, of which waited for: 6 -> 5; matrix products, arithmetic and copies ran while one was open for 21% -> 14% of each run, Pallas kernels for 0% -> 7%
where the time goes in v2:
time: 598 us; the launch traced here: 592 us
  waiting for transfers between devices  266 us (44%)
  Pallas kernels  83.3 us (14%)
  matrix products  76.6 us (13%)
  blocking collectives  70.5 us (12%)
  local copies, waits for them, and re-layouts  54.4 us (9%)
  between operations  17.7 us (3%)
  other arithmetic  14.7 us (2%)
  starting transfers between devices  9.2 us (2%)
    reduce_scatter x5, waiting for transfers between devices, reduced(): share = lax.psum_scatter(grad, 'var', scatter_dimension=0, tiled=True)  220 us
    psum x1, blocking collectives, body(): lax.psum((jnp.concatenate(small), m_part), ('item', 'var'))  59.9 us
    dot_general x16, matrix products, mm(): return jnp.einsum(spec, a, b, preferred_element_type=F32)  49.6 us
    psum x1, waiting for transfers between devices, reduced(): return lax.psum(share, 'item').astype(F32).T  46 us
    pallas_call x1, Pallas kernels, attention_backward_call(): pl.pallas_call(functools.partial(backward_kernel, n), out_shape=(jax.Shap...  43.4 us
    pallas_call x1, Pallas kernels, attention_forward_call(): pl.pallas_call(functools.partial(forward_kernel, n), out_shape=(jax.Shape...  39.9 us
    unnamed x176, local copies, waits for them, and re-layouts  33.3 us
  transfers between devices with their start and end apart: 8, of which 5 were waited for; matrix products, arithmetic and copies ran while one was open for 14% of the time, Pallas kernels for 7%

profile of v2, /device:TPU:0, one launch (start us, length us, event | category | flops | bytes accessed | tf_op | source)
XLA Modules:
  0.0 592.2 jit_solution(12982377601354779721)
XLA Ops:
  7.3 4.0 copy.143
  11.3 4.0 reshape.400
  15.4 5.2 all-to-all-start
  23.6 10.6 %all_gather.3 = bf16[64,5,1024]{2,0,1:T(8,128)(2,1)S(1)} all-gather(bf16[8,5,1024]{2,0,1:T(8,128)(2,1)S(1)} %pad_maximum_fusion), channel_id=1, replica_groups=mesh['item'=4,'var'=8] {'var'}, dimensions={0}, use_global_device_ids=true | all-gather | bytes 737280 | tf_op jit(solution)/shard_map/all_gather | solution.py:418
  34.9 2.4 convolution_convert_fusion.8
  37.3 1.6 reshape.372
  38.9 4.1 copy.142
  43.1 2.5 bitcast_reduce_fusion
  48.0 3.5 reshape.401
  51.4 3.2 copy.144
  57.3 1.5 fusion.70
  60.6 5.8 convolution_convert_fusion.3.qkv
  66.4 39.9 %attention_forward.1 = (bf16[3,2048,128]{2,1,0:T(8,128)(2,1)}, f32[128,2048]{1,0:T(8,128)}, f32[2,2048]{1,0:T(2,128)}, bf16[256,1024]{1,0:T(8,128)(2,1)}) custom-call(bf16[256,3072]{1,0:T(8,128)(2,1)} %convolution_convert_fusion.3.qkv), custom_call_target="tpu_custom_call" | custom-call | flops 40000000000 | bytes 8000000 | tf_op jit(solution)/shard_map/attention_forward/pallas_call | solution.py:316
  106.3 2.0 fusion.75
  108.6 6.5 %multiply_convert_fusion = (bf16[256,4096]{1,0:T(8,128)(2,1)}, f32[256,4096]{1,0:T(8,128)S(1)}) fusion(f32[4096]{0:T(1024)S(1)} %copy-done.59, bf16[1024,4096]{1,0:T(8,128)(2,1)} %param.37, f32[256,1024]{1,0:T(8,128)S(1)} %get-tuple-element.180, f32[1024]{0:T(1024)S(1)} %convert_element_type.179, f32[1024]{0:T(1024)S(1)} %convert_element_type.178, ...), kind=kOutput, calls=%fused_computation.13 | convolution fusion | flops 2155085824 | bytes 15755264 | tf_op jit(solution)/shard_map/dot_general | solution.py:465
  115.2 4.7 convert_reduce_fusion
  120.0 2.7 multiply_reduce_fusion.4
  123.2 1.6 convolution_convert_fusion.7.g_in
  124.7 2.1 convolution_convert_fusion.4
  126.9 43.4 %attention_backward.1 = (bf16[3,2048,128]{2,1,0:T(8,128)(2,1)}, bf16[256,3072]{1,0:T(8,128)(2,1)}) custom-call(bf16[256,1024]{1,0:T(8,128)(2,1)} %convolution_convert_fusion.7.g_in, bf16[3,2048,128]{2,1,0:T(8,128)(2,1)} %get-tuple-element.24.heads, f32[128,2048]{1,0:T(8,128)} %get-tuple-element.25.o_t, f32[2,2048]{1,0:T(2,128)} %get-tuple-element.26.lse), custom_call_target="tpu_custom_call" | custom-call | flops 60000002048 | bytes 8000000 | tf_op jit(solution)/shard_map/attention_backward/pallas_call | solution.py:351
  170.3 5.7 multiply_reduce_fusion.3
  177.0 2.1 convolution_convert_fusion.5
  179.2 4.7 convolution_convert_fusion.2
  185.1 7.4 %convolution_convert_fusion.1 = bf16[4096,1024]{1,0:T(8,128)(2,1)} fusion(bf16[256,4096]{1,0:T(8,128)(2,1)} %copy-done.9, f32[256,1024]{1,0:T(8,128)S(1)} %copy-done.6, f32[1024]{0:T(1024)S(1)} %convert_element_type.179, f32[1024]{0:T(1024)S(1)} %convert_element_type.178, f32[256]{0:T(256)S(1)} %add_rsqrt_fusion, f32[256]{0:T(256)S(1)} %broadcast_multiply_fusion.5), kind=kOutput, calls=%fused_computation.1 | convolution fusion | flops 2152988672 | bytes 11544576 | tf_op jit(solution)/shard_map/rf,rd->fd/dot_general | solution.py:24
  193.5 7.2 %convolution_convert_fusion = bf16[1024,4096]{1,0:T(8,128)(2,1)} fusion(bf16[256,4096]{1,0:T(8,128)(2,1)} %get-tuple-element.181, bf16[1,256,1024]{2,1,0:T(8,128)(2,1)S(1)} %copy-done.14, f32[]{:T(128)S(6)} %div.69), kind=kOutput, calls=%fused_computation | convolution fusion | flops 2152464384 | bytes 11010052 | tf_op jit(solution)/shard_map/rd,rf->df/dot_general | solution.py:24
  204.2 3.1 convolution_convert_fusion.6
  207.3 1.3 copy.147
  209.3 1.9 copy.154
  211.2 2.0 reshape.382
  213.2 1.9 fusion.76
  216.5 1.2 subtract_multiply_fusion.2
  218.4 4.7 reduce-scatter.6.cloned.1.call-done
  223.2 65.2 %reduce-scatter.8.cloned.1.call-done = bf16[384,1024]{1,0:T(8,128)(2,1)} async-done(((bf16[3072,1024]{1,0:T(8,128)(2,1)}), bf16[384,1024]{1,0:T(8,128)(2,1)}) %reduce-scatter.8.cloned.1.call-update) | async-done | bytes 786448 | tf_op jit(solution)/shard_map/reduce_scatter | solution.py:558
  288.4 74.8 %reduce-scatter.12.cloned.1.call-done = bf16[512,1024]{1,0:T(8,128)(2,1)} async-done(((bf16[4096,1024]{1,0:T(8,128)(2,1)}), bf16[512,1024]{1,0:T(8,128)(2,1)}) %reduce-scatter.12.cloned.1.call-update) | async-done | bytes 1048592 | tf_op jit(solution)/shard_map/reduce_scatter | solution.py:558
  363.2 74.8 %reduce-scatter.14.cloned.1.call-done = bf16[128,4096]{1,0:T(8,128)(2,1)} async-done(((bf16[1024,4096]{1,0:T(8,128)(2,1)}), bf16[128,4096]{1,0:T(8,128)(2,1)}) %reduce-scatter.14.cloned.1.call-update) | async-done | bytes 1048592 | tf_op jit(solution)/shard_map/reduce_scatter | solution.py:558
  438.1 59.9 %all-reduce.10 = (f32[13056]{0:T(1024)S(1)}, bf16[240,1024]{1,0:T(8,128)(2,1)}) all-reduce(f32[13056]{0:T(1024)S(1)} %constant_dynamic-update-slice_fusion, f32[240,1024]{1,0:T(8,128)S(1)} %reshape.382), channel_id=1, replica_groups=mesh['item'=4,'var'=8] {'item','var'}, use_global_device_ids=true, to_apply=%region_24.25 | all-reduce | flops 258816 | bytes 1579008 | tf_op jit(solution)/shard_map/psum | solution.py:523
  499.0 2.5 fusion.5
  505.3 3.6 all-to-all-start.1
  511.3 2.5 fusion.27
  515.5 2.9 broadcast_multiply_fusion
  518.4 2.0 fusion.43
  520.4 6.6 %fusion.23 = bf16[1,256,1024]{2,1,0:T(8,128)(2,1)} fusion(f32[256,1024]{1,0:T(8,128)S(1)} %copy-done.6, bf16[256,4096]{1,0:T(8,128)(2,1)S(1)} %copy-done.15, bf16[4096,1024]{1,0:T(8,128)(2,1)} %param.39, f32[1024]{0:T(1024)S(1)} %convert_element_type.183), kind=kOutput, calls=%fused_computation.40 | convolution fusion | flops 2148270080 | bytes 12062720 | tf_op jit(solution)/shard_map/dot_general | solution.py:469
  528.4 46.0 %all-reduce.9.cloned.1.call-done = (bf16[1024,128]{0,1:T(8,128)(2,1)}, bf16[1024,384]{0,1:T(8,128)(2,1)}, bf16[1024,128]{0,1:T(8,128)(2,1)}, bf16[1024,512]{0,1:T(8,128)(2,1)}, bf16[4096,128]{0,1:T(8,128)(2,1)}) async-done(((bf16[1024,128]{0,1:T(8,128)(2,1)}, bf16[1024,384]{0,1:T(8,128)(2,1)}, bf16[1024,128]{0,1:T(8,128)(2,1)}, bf16[1024,512]{0,1:T(8,128)(2,1)}, bf16[4096,128]{0,1:T(8,128)(2,1)}), ...) | async-done | bytes 3407888 | tf_op jit(solution)/shard_map/psum | solution.py:559
  574.4 1.9 copy.158
  576.3 2.0 copy.160
  578.2 2.5 copy.159
  580.8 2.7 copy.161
  583.5 1.6 copy.162
  (262 shorter events, 28.4 us)
Async XLA Ops:
  7.2 99.1 %copy-start = (bf16[1024,1024]{1,0:T(8,128)(2,1)S(1)}, bf16[1024,1024]{1,0:T(8,128)(2,1)}, u32[]{:S(2)}) copy-start(bf16[1024,1024]{1,0:T(8,128)(2,1)} %param.34) | copy-start | bytes 6291460
  7.2 14.1 %copy-start.66 = (bf16[1024]{0:T(1024)(128)(2,1)S(1)}, bf16[1024]{0:T(1024)(128)(2,1)}, u32[]{:S(2)}) copy-start(bf16[1024]{0:T(1024)(128)(2,1)} %param.31) | copy-start | bytes 6148
  7.2 14.1 %copy-start.67 = (bf16[1024]{0:T(1024)(128)(2,1)S(1)}, bf16[1024]{0:T(1024)(128)(2,1)}, u32[]{:S(2)}) copy-start(bf16[1024]{0:T(1024)(128)(2,1)} %param.35) | copy-start | bytes 6148
  7.2 14.1 %copy-start.68 = (bf16[1024]{0:T(1024)(128)(2,1)S(1)}, bf16[1024]{0:T(1024)(128)(2,1)}, u32[]{:S(2)}) copy-start(bf16[1024]{0:T(1024)(128)(2,1)} %param.32) | copy-start | bytes 6148
  7.2 14.1 %copy-start.69 = (bf16[1024]{0:T(1024)(128)(2,1)S(1)}, bf16[1024]{0:T(1024)(128)(2,1)}, u32[]{:S(2)}) copy-start(bf16[1024]{0:T(1024)(128)(2,1)} %param.36) | copy-start | bytes 6148
  7.2 14.1 %copy-start.61 = (s32[5,64]{1,0:T(8,128)S(1)}, s32[5,64]{1,0:T(8,128)}, u32[]{:S(2)}) copy-start(s32[5,64]{1,0:T(8,128)} %param.23) | copy-start | bytes 3844
  7.3 14.1 %copy-start.70 = (bf16[1024]{0:T(1024)(128)(2,1)S(1)}, bf16[1024]{0:T(1024)(128)(2,1)}, u32[]{:S(2)}) copy-start(bf16[1024]{0:T(1024)(128)(2,1)} %param.27) | copy-start | bytes 6148
  7.3 14.7 %copy-start.60 = (bf16[4096]{0:T(1024)(128)(2,1)S(1)}, bf16[4096]{0:T(1024)(128)(2,1)}, u32[]{:S(2)}) copy-start(bf16[4096]{0:T(1024)(128)(2,1)} %param.38) | copy-start | bytes 24580
  7.3 16.3 %copy-start.54 = (bf16[8,4,1024]{2,1,0:T(4,128)(2,1)S(1)}, bf16[8,4,1024]{2,1,0:T(4,128)(2,1)}, u32[]{:S(2)}) copy-start(bf16[8,4,1024]{2,1,0:T(4,128)(2,1)} %param.25) | copy-start | bytes 196612
  7.3 16.3 %copy-start.58 = (bf16[8,1024]{1,0:T(8,128)(2,1)S(1)}, bf16[8,1024]{1,0:T(8,128)(2,1)}, u32[]{:S(2)}) copy-start(bf16[8,1024]{1,0:T(8,128)(2,1)} %param.26) | copy-start | bytes 49156
  15.4 32.6 %all-to-all-start = ((bf16[8,2,4096]{2,1,0:T(2,128)(2,1)}), bf16[8,2,4096]{2,1,0:T(2,128)(2,1)S(1)}, u32[]{:S(2)}, u32[]{:S(2)}) async-start(bf16[8,2,4096]{2,1,0:T(2,128)(2,1)} %reshape.400), calls=%async_computation | async-start | bytes 262144 | tf_op jit(solution)/shard_map/all_to_all | solution.py:421
  20.6 197.9 %reduce-scatter.10.cloned.1.call-start = ((), (), s32[]{:S(2)}) async-start(), calls=%async_computation.9 | async-start | bytes 2359296 | tf_op jit(solution)/shard_map/reduce_scatter | solution.py:558
  34.9 10.7 %copy-start.7 = (bf16[48,5,1024]{2,0,1:T(8,128)(2,1)}, bf16[48,5,1024]{2,0,1:T(8,128)(2,1)S(1)}, u32[]{:S(2)}) copy-start(bf16[48,5,1024]{2,0,1:T(8,128)(2,1)S(1)} %reshape.370) | copy-start | bytes 1474564
  37.3 5.7 copy-start.57
  38.9 7.0 %copy-start.72 = (s32[5]{0:T(128)S(1)}, s32[5]{0:T(128)}, u32[]{:S(2)}) copy-start(s32[5]{0:T(128)} %param.24) | copy-start | bytes 64
  38.9 9.0 %copy-start.64 = (f32[48]{0:T(128)S(1)}, f32[48]{0:T(128)}, u32[]{:S(2)}) copy-start(f32[48]{0:T(128)} %broadcast_in_dim_reshape.3) | copy-start | bytes 580
  45.6 5.9 copy-start.40
  45.9 5.5 copy-start.39
  45.9 11.3 %copy-start.42 = (f32[16,48]{1,0:T(8,128)}, f32[16,48]{1,0:T(8,128)S(1)}, u32[]{:S(2)}) copy-start(f32[16,48]{1,0:T(8,128)S(1)} %get-tuple-element.172) | copy-start | bytes 9220
  45.9 11.3 %copy-start.44 = (f32[16,48]{1,0:T(8,128)}, f32[16,48]{1,0:T(8,128)S(1)}, u32[]{:S(2)}) copy-start(f32[16,48]{1,0:T(8,128)S(1)} %get-tuple-element.173) | copy-start | bytes 9220
  45.9 11.3 %copy-start.46 = (f32[16,48]{1,0:T(8,128)}, f32[16,48]{1,0:T(8,128)S(1)}, u32[]{:S(2)}) copy-start(f32[16,48]{1,0:T(8,128)S(1)} %get-tuple-element.174) | copy-start | bytes 9220
  45.9 11.3 %copy-start.48 = (f32[16,48]{1,0:T(8,128)}, f32[16,48]{1,0:T(8,128)S(1)}, u32[]{:S(2)}) copy-start(f32[16,48]{1,0:T(8,128)S(1)} %get-tuple-element.175) | copy-start | bytes 9220
  46.0 11.3 %copy-start.50 = (f32[16,48]{1,0:T(8,128)}, f32[16,48]{1,0:T(8,128)S(1)}, u32[]{:S(2)}) copy-start(f32[16,48]{1,0:T(8,128)S(1)} %get-tuple-element.176) | copy-start | bytes 9220
  47.9 9.4 %copy-start.62 = (pred[48]{0:T(512)(128)(4,1)}, pred[48]{0:T(512)(128)(4,1)S(1)}, u32[]{:S(2)}) copy-start(pred[48]{0:T(512)(128)(4,1)S(1)} %broadcast_compare_fusion) | copy-start | bytes 148
  51.4 7.5 %copy-start.10 = (bf16[5,48,16,64]{3,2,1,0:T(8,128)(2,1)S(1)}, bf16[5,48,16,64]{3,2,1,0:T(8,128)(2,1)}, u32[]{:S(2)}) copy-start(bf16[5,48,16,64]{3,2,1,0:T(8,128)(2,1)} %reshape.372) | copy-start | bytes 1474564
  55.5 4.7 copy-start.27
  106.3 8.9 %slice-start.3 = ((s8[8388608]{0:T(1024)(128)(4,1)}), s8[4194304]{0:T(1024)(128)(4,1)S(1)}, s32[]{:S(2)}) async-start(s8[8388608]{0:T(1024)(128)(4,1)} %bitcast.203), calls=%async_computation.16 | async-start | bytes 8388608
  108.3 14.4 %copy-start.5 = (f32[256,1024]{1,0:T(8,128)}, f32[256,1024]{1,0:T(8,128)S(1)}, u32[]{:S(2)}) copy-start(f32[256,1024]{1,0:T(8,128)S(1)} %get-tuple-element.180) | copy-start | bytes 3145732
  108.6 6.6 %copy-start.13 = (bf16[1,256,1024]{2,1,0:T(8,128)(2,1)S(1)}, bf16[1,256,1024]{2,1,0:T(8,128)(2,1)}, u32[]{:S(2)}) copy-start(bf16[1,256,1024]{2,1,0:T(8,128)(2,1)} %param.41) | copy-start | bytes 1572868
  108.6 6.6 %slice-start.4 = ((s8[8388608]{0:T(1024)(128)(4,1)}), s8[4194304]{0:T(1024)(128)(4,1)S(1)}, s32[]{:S(2)}) async-start(s8[8388608]{0:T(1024)(128)(4,1)} %bitcast.203), calls=%async_computation.17 | async-start | bytes 8388608
  108.6 11.3 %slice-start.1 = ((s8[8388608]{0:T(1024)(128)(4,1)}), s8[4194304]{0:T(1024)(128)(4,1)S(1)}, s32[]{:S(2)}) async-start(s8[8388608]{0:T(1024)(128)(4,1)} %bitcast.201), calls=%async_computation.14 | async-start | bytes 8388608
  115.2 4.8 slice-start.2
  126.8 96.4 %reduce-scatter.6.cloned.1.call-start = ((), (), s32[]{:S(2)}) async-start(), calls=%async_computation.7 | async-start | bytes 2359296 | tf_op jit(solution)/shard_map/reduce_scatter | solution.py:558
  170.3 5.7 copy-start.4
  177.0 6.8 %copy-start.18 = (bf16[256,1024]{1,0:T(8,128)(2,1)}, bf16[256,1024]{1,0:T(8,128)(2,1)S(1)}, u32[]{:S(2)}) copy-start(bf16[256,1024]{1,0:T(8,128)(2,1)S(1)} %add_convert_fusion) | copy-start | bytes 1572868
  179.1 109.2 %reduce-scatter.8.cloned.1.call-start = ((), (), s32[]{:S(2)}) async-start(), calls=%async_computation.8 | async-start | bytes 7077888 | tf_op jit(solution)/shard_map/reduce_scatter | solution.py:558
  183.9 179.3 %reduce-scatter.12.cloned.1.call-start = ((), (), s32[]{:S(2)}) async-start(), calls=%async_computation.10 | async-start | bytes 9437184 | tf_op jit(solution)/shard_map/reduce_scatter | solution.py:558
  192.5 245.5 %reduce-scatter.14.cloned.1.call-start = ((), (), s32[]{:S(2)}) async-start(), calls=%async_computation.11 | async-start | bytes 9437184 | tf_op jit(solution)/shard_map/reduce_scatter | solution.py:558
  200.8 373.5 %all-reduce.9.cloned.1.call-start = ((), (), s32[]{:S(2)}) async-start(), calls=%async_computation.12 | async-start | bytes 6815744 | tf_op jit(solution)/shard_map/psum | solution.py:559
  203.2 5.4 copy-start.24
  203.2 5.4 copy-start.28
  498.6 10.3 %copy-start.26 = (bf16[240,1024]{1,0:T(8,128)(2,1)S(1)}, bf16[240,1024]{1,0:T(8,128)(2,1)}, u32[]{:S(2)}) copy-start(bf16[240,1024]{1,0:T(8,128)(2,1)} %get-tuple-element.147) | copy-start | bytes 1474564
  501.5 9.5 %copy-start.41 = (bf16[1024,16]{0,1:T(8,128)(2,1)S(1)}, bf16[1024,16]{0,1:T(8,128)(2,1)}, u32[]{:S(2)}) copy-start(bf16[1024,16]{0,1:T(8,128)(2,1)} %copy-done.40) | copy-start | bytes 98308
  505.3 22.4 %all-to-all-start.1 = ((bf16[1,64,4,256]{3,2,0,1:T(4,128)(2,1)}), bf16[1,64,4,256]{3,2,0,1:T(4,128)(2,1)S(1)}, u32[]{:S(2)}, u32[]{:S(2)}) async-start(bf16[1,64,4,256]{3,2,0,1:T(4,128)(2,1)} %bitcast.41), calls=%async_computation.1 | async-start | bytes 262144 | tf_op jit(solution)/shard_map/all_to_all | solution.py:509
  509.5 5.8 copy-start.8
  511.0 9.4 %copy-start.15 = (bf16[256,4096]{1,0:T(8,128)(2,1)S(1)}, bf16[256,4096]{1,0:T(8,128)(2,1)}, u32[]{:S(2)}) copy-start(bf16[256,4096]{1,0:T(8,128)(2,1)} %get-tuple-element.181) | copy-start | bytes 6291460
  576.3 7.2 %copy-start.25 = (bf16[4096,128]{0,1:T(8,128)(2,1)S(1)}, bf16[4096,128]{0,1:T(8,128)(2,1)}, u32[]{:S(2)}) copy-start(bf16[4096,128]{0,1:T(8,128)(2,1)} %get-tuple-element.152) | copy-start | bytes 3145732
  580.8 4.3 copy-start.1
  (38 other events, 73.3 us)
Sparse Core Ops, SparseCore 0:
  126.9 51.2 reduce-scatter.9
  182.1 41.0 reduce-scatter.5
  226.6 61.7 reduce-scatter.7
  291.7 71.4 reduce-scatter.11
  366.5 71.4 reduce-scatter.13
  440.7 133.6 all-reduce.8
